TPU v7x, 32 devices: a whole 2x2x4 slice. The times are simulated.
32 devices in a mesh: dp: 4 (over y, core), ctx: 4 (over z), tensor: 2 (over x).
Axes of the slice: x: 2, y: 2, z: 4, core: 2. Of those that a mesh axis runs over, the one named last changes fastest.
Arguments:
- layer_input: bfloat16 [12, 1024, 1536], P('dp', 'ctx'), may hold values from -6 to 6
- cotangent: float32 [12, 1024, 1536], P('dp', 'ctx', 'tensor'), may hold values from -6 to 6
- in_proj: float32 [1536, 2, 3072], P(('dp', 'ctx'), None, 'tensor'), may hold values from -0.15625 to 0.15625
- delta_proj: float32 [1536, 48], P(('dp', 'ctx'), 'tensor'), may hold values from -0.21875 to 0.21875
- out_proj: float32 [1536, 3072], P(('dp', 'ctx'), 'tensor'), may hold values from -0.109375 to 0.109375
- state_proj: float32 [1536, 2, 128], P(('dp', 'ctx', 'tensor')), may hold values from -0.15625 to 0.15625
- packed_params: float32 [21408], P(('dp', 'ctx', 'tensor')), may hold values from -6 to 6
- moment_in: float32 [1536, 2, 3072], P(('dp', 'ctx'), None, 'tensor'), may hold values from -18 to 18
- moment_delta: float32 [1536, 48], P(('dp', 'ctx'), 'tensor'), may hold values from -18 to 18
- moment_out: float32 [1536, 3072], P(('dp', 'ctx'), 'tensor'), may hold values from -18 to 18
- moment_state: float32 [1536, 2, 128], P(('dp', 'ctx', 'tensor')), may hold values from -18 to 18
- moment_packed: float32 [21408], P(('dp', 'ctx', 'tensor')), may hold values from -18 to 18
- square_in: float32 [1536, 2, 3072], P(('dp', 'ctx'), None, 'tensor'), may hold values from 1 to 30
- square_delta: float32 [1536, 48], P(('dp', 'ctx'), 'tensor'), may hold values from 1 to 30
- square_out: float32 [1536, 3072], P(('dp', 'ctx'), 'tensor'), may hold values from 1 to 30
- square_state: float32 [1536, 2, 128], P(('dp', 'ctx', 'tensor')), may hold values from 1 to 30
- square_packed: float32 [21408], P(('dp', 'ctx', 'tensor')), may hold values from 1 to 30
Outputs:
- layer_output: float32 [12, 1024, 1536], P('dp', 'ctx', 'tensor')
- input_grad: float32 [12, 1024, 1536], P('dp', 'ctx', 'tensor')
- grad_in: float32 [1536, 2, 3072], P(('dp', 'ctx'), None, 'tensor')
- grad_delta: float32 [1536, 48], P(('dp', 'ctx'), 'tensor')
- grad_out: float32 [1536, 3072], P(('dp', 'ctx'), 'tensor')
- grad_state: float32 [1536, 2, 128], P(('dp', 'ctx', 'tensor'))
- grad_packed: float32 [21408], P(('dp', 'ctx', 'tensor'))
- new_in: float32 [1536, 2, 3072], P(('dp', 'ctx'), None, 'tensor')
- new_delta: float32 [1536, 48], P(('dp', 'ctx'), 'tensor')
- new_out: float32 [1536, 3072], P(('dp', 'ctx'), 'tensor')
- new_state: float32 [1536, 2, 128], P(('dp', 'ctx', 'tensor'))
- new_packed: float32 [21408], P(('dp', 'ctx', 'tensor'))
- next_moment_in: float32 [1536, 2, 3072], P(('dp', 'ctx'), None, 'tensor')
- next_moment_delta: float32 [1536, 48], P(('dp', 'ctx'), 'tensor')
- next_moment_out: float32 [1536, 3072], P(('dp', 'ctx'), 'tensor')
- next_moment_state: float32 [1536, 2, 128], P(('dp', 'ctx', 'tensor'))
- next_moment_packed: float32 [21408], P(('dp', 'ctx', 'tensor'))
- next_square_in: float32 [1536, 2, 3072], P(('dp', 'ctx'), None, 'tensor')
- next_square_delta: float32 [1536, 48], P(('dp', 'ctx'), 'tensor')
- next_square_out: float32 [1536, 3072], P(('dp', 'ctx'), 'tensor')
- next_square_state: float32 [1536, 2, 128], P(('dp', 'ctx', 'tensor'))
- next_square_packed: float32 [21408], P(('dp', 'ctx', 'tensor'))
All inputs are finite; a program needn't handle non-finite values.
Results may differ from a plain program's by a relative error of at most 0.00105.
The roundings to bfloat16 on the way count: a program that leaves them out, or rounds other values in their place, can miss the bound.
Values may be sent and summed in bfloat16 or wider, within the bound.
A program may use at most 256 MiB of HBM per device.

v0:
```python
import functools

import jax
import jax.numpy as jnp
from jax import lax
from jax.experimental import pallas as pl
from jax.experimental.pallas import tpu as pltpu
from jax.sharding import PartitionSpec as P


D = 1536
HEADS = 48
HEAD_DIM = 64
STATE = 128
CONV = 4
STEP = 3
INNER = 3072
LANES = 128

NORM_EPS = 1e-05
BETA_ONE = 0.9
BETA_TWO = 0.999
ADAM_EPS = 1e-08
DECAY_RATE = 0.1
MATRIX_RATE = 0.01
PACKED_RATE = 0.1
HIGH = lax.Precision.HIGHEST
MESH = pl.DeviceIdType.MESH
BF = jnp.bfloat16
F32 = jnp.float32


def cdiv(a, b):
    return -(-a // b)


def gather_kernel(sizes, in_ref, out_ref, local_sem, send_sem, recv_sem):
    n_dp, n_ctx, n_t = sizes
    d, c, t = lax.axis_index("dp"), lax.axis_index("ctx"), lax.axis_index("tensor")
    peers = []
    for k in range(1, n_ctx):
        peers.append((d, lax.rem(c + k, n_ctx), t))
    for k in range(1, n_t):
        peers.append((d, c, lax.rem(t + k, n_t)))
    for k in range(1, n_dp):
        peers.append((lax.rem(d + k, n_dp), c, t))
    barrier = pltpu.get_barrier_semaphore()
    for peer in peers:
        pl.semaphore_signal(barrier, inc=1, device_id=peer, device_id_type=MESH)
    pl.semaphore_wait(barrier, len(peers))
    own = pltpu.make_async_copy(in_ref, out_ref.at[d, c, t], local_sem)
    own.start()
    own.wait()
    number = 0

    def stage(copies):
        for copy in copies:
            copy.start()
        for copy in copies:
            copy.wait()

    copies = []
    for k in range(1, n_ctx):
        view = out_ref.at[d, c, t]
        copies.append(
            pltpu.make_async_remote_copy(
                src_ref=view,
                dst_ref=view,
                send_sem=send_sem.at[number],
                recv_sem=recv_sem.at[number],
                device_id=(d, lax.rem(c + k, n_ctx), t),
                device_id_type=MESH,
            )
        )
        number += 1
    stage(copies)
    copies = []
    for k in range(1, n_t):
        view = out_ref.at[d, :, t]
        copies.append(
            pltpu.make_async_remote_copy(
                src_ref=view,
                dst_ref=view,
                send_sem=send_sem.at[number],
                recv_sem=recv_sem.at[number],
                device_id=(d, c, lax.rem(t + k, n_t)),
                device_id_type=MESH,
            )
        )
        number += 1
    stage(copies)
    copies = []
    for k in range(1, n_dp):
        view = out_ref.at[d]
        copies.append(
            pltpu.make_async_remote_copy(
                src_ref=view,
                dst_ref=view,
                send_sem=send_sem.at[number],
                recv_sem=recv_sem.at[number],
                device_id=(lax.rem(d + k, n_dp), c, t),
                device_id_type=MESH,
            )
        )
        number += 1
    stage(copies)


def gather_small(block, sizes):
    count = sum(sizes) - 3
    return pl.pallas_call(
        functools.partial(gather_kernel, sizes),
        out_shape=jax.ShapeDtypeStruct(sizes + block.shape, block.dtype),
        in_specs=[pl.BlockSpec(memory_space=pltpu.VMEM)],
        out_specs=pl.BlockSpec(memory_space=pltpu.VMEM),
        scratch_shapes=[
            pltpu.SemaphoreType.DMA(()),
            pltpu.SemaphoreType.DMA((count,)),
            pltpu.SemaphoreType.DMA((count,)),
        ],
        compiler_params=pltpu.CompilerParams(collective_id=0, has_side_effects=True),
        name="gather_small",
    )(block)


PAIR = LANES // HEAD_DIM


def step_width(inner):
    return 3 * LANES if inner % (3 * LANES) == 0 else LANES


def matmul(left, right, contract):
    return lax.dot_general(
        left, right, ((contract[:1], contract[1:]), ((), ())), preferred_element_type=F32
    )


def split(value):
    high = value.astype(BF)
    return high, (value - high.astype(F32)).astype(BF)


def dot_exact_right(left, right, contract):
    high, low = split(left)
    return matmul(high, right, contract) + matmul(low, right, contract)


def dot_exact_left(left, right, contract):
    high, low = split(right)
    return matmul(left, high, contract) + matmul(left, low, contract)


def dot_terms(left, right, contract):
    left_high, left_low = split(left)
    right_high, right_low = split(right)
    return (
        matmul(left_high, right_high, contract)
        + matmul(left_high, right_low, contract)
        + matmul(left_low, right_high, contract)
    )


def picker(heads, first, width, each):
    row = lax.broadcasted_iota(jnp.int32, (heads, width), 0)
    lane = lax.broadcasted_iota(jnp.int32, (heads, width), 1)
    return jnp.where(row == first + lane // each, 1.0, 0.0).astype(BF)


def spread_exact(values, first, width, each):
    pick = picker(values.shape[1], first, width, each)
    high = values.astype(BF)
    rest = values - high.astype(F32)
    middle = rest.astype(BF)
    low = (rest - middle.astype(F32)).astype(BF)
    return matmul(high, pick, (1, 0)) + (matmul(middle, pick, (1, 0)) + matmul(low, pick, (1, 0)))


def place_heads(values, first, heads):
    width = values.shape[1]
    lane = lax.broadcasted_iota(jnp.int32, (width, heads), 0)
    column = lax.broadcasted_iota(jnp.int32, (width, heads), 1)
    pick = jnp.where(column == first + lane // HEAD_DIM, 1.0, 0.0).astype(BF)
    return dot_exact_right(values, pick, (1, 0))


def twice(value, wide):
    count = wide // LANES
    return value if count <= 1 else jnp.concatenate([value] * count, axis=1)


def state_kernel(v_ref, u_ref, scale_ref, out_ref):
    width = v_ref.shape[2]
    first = pl.program_id(0) * (width // HEAD_DIM)
    scaled = v_ref[0].astype(F32) * spread_exact(scale_ref[0], first, width, HEAD_DIM)
    out_ref[...] = dot_exact_right(scaled, u_ref[0], (0, 0))


def within_kernel(x_ref, w_ref, r_ref, cum_ref, cum_t_ref, delta_t_ref, out_ref, score_ref, down_ref):
    step = pl.program_id(1)
    tokens, width = x_ref.shape[1:]
    edge = min(tokens, LANES)
    count = width // HEAD_DIM
    first = step * count

    @pl.when(step == 0)
    def _():
        score_ref[...] = matmul(r_ref[0], w_ref[0], (1, 1))

    down_ref[...] = spread_exact(cum_ref[0], first, count * LANES, LANES)
    lanes = lax.broadcasted_iota(jnp.int32, (edge, LANES), 1)
    for top in range(0, tokens, edge):
        wide = top + edge
        rows_at = top + lax.broadcasted_iota(jnp.int32, (edge, wide), 0)
        causal = rows_at >= lax.broadcasted_iota(jnp.int32, (edge, wide), 1)
        score = score_ref[top:wide, :wide]
        for tile in range(width // LANES):
            channels = slice(tile * LANES, (tile + 1) * LANES)
            x = x_ref[0, :wide, channels]
            result = None
            for k in range(PAIR):
                at = tile * PAIR + k
                down = twice(down_ref[top:wide, at * LANES : (at + 1) * LANES], wide)
                across = cum_t_ref[0, pl.ds(first + at, 1), :][:, :wide]
                scale = delta_t_ref[0, pl.ds(first + at, 1), :][:, :wide]
                decays = jnp.exp(jnp.where(causal, down - across, -1e30))
                part = dot_exact_right(decays * (score * scale), x, (1, 0))
                result = part if k == 0 else jnp.where(lanes < k * HEAD_DIM, result, part)
            out_ref[0, top:wide, channels] = result


def gate_kernel(
    within_ref, x_ref, z_ref, r_ref, growth_ref, enter_ref, skip_ref, plain_ref, mixed_ref, sum_ref
):
    step = pl.program_id(1)
    width = x_ref.shape[2]
    first = step * (width // HEAD_DIM)
    carried = dot_exact_left(r_ref[0], enter_ref[0], (1, 1))
    plain = within_ref[0] + carried * spread_exact(growth_ref[0], first, width, HEAD_DIM)
    plain_ref[0] = plain
    gate = z_ref[0].astype(F32)
    mixed = (plain + skip_ref[...] * x_ref[0].astype(F32)) * (gate * jax.nn.sigmoid(gate))
    mixed_ref[0] = mixed

    @pl.when(step == 0)
    def _():
        sum_ref[...] = jnp.zeros_like(sum_ref)

    sum_ref[0] += jnp.sum(mixed * mixed, axis=1, keepdims=True)


def within_back_kernel(
    dy_ref, x_ref, w_ref, r_ref, cum_ref, cum_t_ref, delta_ref, bare_ref, dw_ref, dr_ref,
    score_ref, total_ref, down_ref, scale_ref,
):
    step = pl.program_id(1)
    tokens, width = x_ref.shape[1:]
    edge = min(tokens, LANES)
    count = width // HEAD_DIM
    first = step * count

    @pl.when(step == 0)
    def _():
        score_ref[...] = matmul(w_ref[0], r_ref[0], (1, 1))
        total_ref[...] = jnp.zeros_like(total_ref)

    down_ref[...] = spread_exact(cum_ref[0], first, count * LANES, LANES)
    scale_ref[...] = spread_exact(delta_ref[0], first, count * LANES, LANES)
    for top in range(0, tokens, edge):
        wide = tokens - top
        rows_at = lax.broadcasted_iota(jnp.int32, (edge, wide), 0)
        causal = rows_at <= lax.broadcasted_iota(jnp.int32, (edge, wide), 1)
        lanes = lax.broadcasted_iota(jnp.int32, (wide, LANES), 1)
        near = lax.broadcasted_iota(jnp.int32, (edge, LANES), 1)
        score = score_ref[top : top + edge, top:]
        added = None
        for tile in range(width // LANES):
            channels = slice(tile * LANES, (tile + 1) * LANES)
            x = x_ref[0, top : top + edge, channels]
            dy_high, dy_low = split(dy_ref[0, top:, channels])
            zero = jnp.zeros_like(dy_high)
            result = None
            for k in range(PAIR):
                at = tile * PAIR + k
                down = twice(down_ref[top : top + edge, at * LANES : (at + 1) * LANES], wide)
                scale = twice(scale_ref[top : top + edge, at * LANES : (at + 1) * LANES], wide)
                across = cum_t_ref[0, pl.ds(first + at, 1), :][:, top:]
                decays = jnp.exp(jnp.where(causal, across - down, -1e30))
                high, low = split(decays * score)
                part = matmul(high, dy_high, (1, 0)) + matmul(high, dy_low, (1, 0))
                part = part + matmul(low, dy_high, (1, 0))
                result = part if k == 0 else jnp.where(near < k * HEAD_DIM, result, part)
                mine = (lanes >= k * HEAD_DIM) & (lanes < (k + 1) * HEAD_DIM)
                pairs = matmul(x, jnp.where(mine, dy_high, zero), (1, 1))
                pairs = pairs + matmul(x, jnp.where(mine, dy_low, zero), (1, 1))
                term = pairs * decays * scale
                added = term if added is None else added + term
            bare_ref[0, top : top + edge, channels] = result
        total_ref[top : top + edge, top:] += added

    @pl.when(step == pl.num_programs(1) - 1)
    def _():
        high, low = split(total_ref[...])
        dw_ref[0] = matmul(high, r_ref[0], (1, 0)) + matmul(low, r_ref[0], (1, 0))
        dr_ref[0] = matmul(high, w_ref[0], (0, 0)) + matmul(low, w_ref[0], (0, 0))


def state_back_kernel(
    dy_ref, x_ref, plain_ref, bare_ref, w_ref, delta_ref, fading_ref, growth_ref, enter_ref,
    leave_ref, skip_ref, dw_in_ref, dr_in_ref, dx_ref, dw_ref, dr_ref, bare_dot_ref, fade_dot_ref,
    plain_dot_ref, skip_dot_ref,
):
    step = pl.program_id(1)
    width = x_ref.shape[2]
    first = step * (width // HEAD_DIM)
    heads = delta_ref.shape[2]

    @pl.when(step == 0)
    def _():
        dw_ref[...] = dw_in_ref[...]
        dr_ref[...] = dr_in_ref[...]
        bare_dot_ref[...] = jnp.zeros_like(bare_dot_ref)
        fade_dot_ref[...] = jnp.zeros_like(fade_dot_ref)
        plain_dot_ref[...] = jnp.zeros_like(plain_dot_ref)

    x = x_ref[0].astype(F32)
    dy = dy_ref[0]
    bare = bare_ref[0]
    fading = spread_exact(fading_ref[0], first, width, HEAD_DIM)
    reach = dot_exact_left(w_ref[0], leave_ref[0], (1, 1))
    dx_ref[0] = (
        spread_exact(delta_ref[0], first, width, HEAD_DIM) * bare
        + fading * reach
        + skip_ref[...] * dy
    )
    growth = spread_exact(growth_ref[0], first, width, HEAD_DIM)
    dr_ref[0] += dot_terms(dy * growth, enter_ref[0], (1, 0))
    dw_ref[0] += dot_terms(x * fading, leave_ref[0], (1, 0))
    bare_dot_ref[0] += place_heads(x * bare, first, heads)
    fade_dot_ref[0] += place_heads(x * reach, first, heads)
    plain_dot_ref[0] += place_heads(dy * plain_ref[0], first, heads)
    skip_dot_ref[0] = jnp.sum(dy * x, axis=0, keepdims=True)


def scan_specs(tokens, inner, heads):
    width = step_width(inner)
    tile = pl.BlockSpec((1, tokens, width), lambda s, j: (s, 0, j))
    state = pl.BlockSpec((1, tokens, STATE), lambda s, j: (s, 0, 0))
    per_head = pl.BlockSpec((1, tokens, heads), lambda s, j: (s, 0, 0))
    per_head_t = pl.BlockSpec((1, heads, tokens), lambda s, j: (s, 0, 0))
    carry = pl.BlockSpec((1, width, STATE), lambda s, j: (s, j, 0))
    lane = pl.BlockSpec((1, width), lambda s, j: (0, j))
    one = pl.BlockSpec((1, tokens, 1), lambda s, j: (s, 0, 0))
    lane_sum = pl.BlockSpec((1, 1, width), lambda s, j: (s, 0, j))
    return tile, state, per_head, per_head_t, carry, lane, one, lane_sum


def shaped(*shape):
    return jax.ShapeDtypeStruct(shape, F32)


def scan_call(kernel, grid, in_specs, out_specs, out_shape, scratch, flops, moved):
    return pl.pallas_call(
        kernel,
        grid=grid,
        in_specs=in_specs,
        out_specs=out_specs,
        out_shape=out_shape,
        scratch_shapes=scratch,
        cost_estimate=pl.CostEstimate(flops=flops, bytes_accessed=moved, transcendentals=0),
    )


def scan_state(v, u, scale, s):
    _, tokens, inner = v.shape
    heads = scale.shape[2]
    width = step_width(inner)
    return scan_call(
        state_kernel, (inner // width,),
        [
            pl.BlockSpec((1, tokens, width), lambda j: (s, 0, j)),
            pl.BlockSpec((1, tokens, STATE), lambda j: (s, 0, 0)),
            pl.BlockSpec((1, tokens, heads), lambda j: (s, 0, 0)),
        ],
        pl.BlockSpec((width, STATE), lambda j: (j, 0)), shaped(inner, STATE),
        [], 4 * tokens * inner * STATE, 8 * tokens * inner,
    )(v, u, scale)


def scan_within(x, w, r, cum, cum_t, delta_t):
    seqs, tokens, inner = x.shape
    width = step_width(inner)
    tile, state, per_head, per_head_t, _, _, _, _ = scan_specs(tokens, inner, cum.shape[2])
    size = seqs * tokens * inner
    return scan_call(
        within_kernel, (seqs, inner // width),
        [tile, state, state, per_head, per_head_t, per_head_t], tile, shaped(seqs, tokens, inner),
        [pltpu.VMEM((tokens, tokens), F32), pltpu.VMEM((tokens, PAIR * width), F32)],
        16 * size * tokens, 6 * size,
    )(x, w, r, cum, cum_t, delta_t)


def scan_gate(within, x, z, r, growth, enter, skip):
    seqs, tokens, inner = x.shape
    tile, state, per_head, _, carry, lane, one, _ = scan_specs(tokens, inner, growth.shape[2])
    size = seqs * tokens * inner
    return scan_call(
        gate_kernel, (seqs, inner // step_width(inner)),
        [tile, tile, tile, state, per_head, carry, lane], [tile, tile, one],
        [shaped(seqs, tokens, inner), shaped(seqs, tokens, inner), shaped(seqs, tokens, 1)],
        [], 8 * size * STATE, 16 * size,
    )(within, x, z, r, growth, enter, skip)


def scan_within_back(dy, x, w, r, cum, cum_t, delta):
    seqs, tokens, inner = x.shape
    width = step_width(inner)
    tile, state, per_head, per_head_t, _, _, _, _ = scan_specs(tokens, inner, cum.shape[2])
    size = seqs * tokens * inner
    square = pltpu.VMEM((tokens, tokens), F32)
    wide = pltpu.VMEM((tokens, PAIR * width), F32)
    return scan_call(
        within_back_kernel, (seqs, inner // width),
        [tile, tile, state, state, per_head, per_head_t, per_head], [tile, state, state],
        [shaped(seqs, tokens, inner), shaped(seqs, tokens, STATE), shaped(seqs, tokens, STATE)],
        [square, square, wide, wide], 32 * size * tokens, 10 * size,
    )(dy, x, w, r, cum, cum_t, delta)


def scan_state_back(dy, x, plain, bare, w, delta, fading, growth, enter, leave, skip, dw, dr):
    seqs, tokens, inner = x.shape
    heads = delta.shape[2]
    tile, state, per_head, _, carry, lane, _, lane_sum = scan_specs(tokens, inner, heads)
    size = seqs * tokens * inner
    sums = shaped(seqs, tokens, heads)
    return scan_call(
        state_back_kernel, (seqs, inner // step_width(inner)),
        [tile] * 4 + [state] + [per_head] * 3 + [carry, carry, lane, state, state],
        [tile, state, state, per_head, per_head, per_head, lane_sum],
        [shaped(seqs, tokens, inner), shaped(seqs, tokens, STATE), shaped(seqs, tokens, STATE)]
        + [sums] * 3 + [shaped(seqs, 1, inner)],
        [], 24 * size * STATE, 22 * size,
    )(dy, x, plain, bare, w, delta, fading, growth, enter, leave, skip, dw, dr)


def from_behind(value, axis, steps):
    count = lax.axis_size(axis)
    initial, last = (max(0, -steps), min(count, count - steps))
    return lax.ppermute(value, axis, [(source, source + steps) for source in range(initial, last)])


def swap(value):
    return lax.ppermute(value, "tensor", [(0, 1), (1, 0)])


def sum_tensor(value):
    if lax.axis_size("tensor") == 2:
        return value + swap(value)
    return lax.psum(value, "tensor")


def scatter_tensor(make, width, rank):
    if lax.axis_size("tensor") == 2:
        away = swap(make((1 - rank) * width))
        return make(rank * width), away
    whole = jnp.concatenate([make(k * width) for k in range(lax.axis_size("tensor"))], axis=-1)
    return lax.psum_scatter(whole, "tensor", scatter_dimension=whole.ndim - 1, tiled=True), 0.0


def over_dp(value, flip):
    return lax.ppermute(value, "dp", [(k, k ^ flip) for k in range(lax.axis_size("dp"))])


def row_blocks(width):
    d = lax.axis_index("dp")
    return lax.rem(d, 2), d // 2, width // lax.axis_size("dp")


def staged():
    return lax.axis_size("dp") == 4


def cut_dot(left, right):
    def part(start, rows):
        return dot(lax.dynamic_slice_in_dim(left, start, rows, 1), right, (0, 0))

    return part


def scatter_start(part, width):
    if not staged():
        return ()
    low, high, rows = row_blocks(width)
    first = part((2 * (1 - high) + 1 - low) * rows, rows)
    second = part((2 * high + 1 - low) * rows, rows)
    return over_dp(first, 1), over_dp(second, 1)


def scatter_high(part, width, near):
    if not staged():
        return ()
    low, high, rows = row_blocks(width)
    return over_dp(part((2 * (1 - high) + low) * rows, rows) + near[0], 2)


def scatter_end(part, width, near, far):
    if not staged():
        return lax.psum_scatter(
            part(0, width), ("dp", "ctx"), scatter_dimension=0, tiled=True
        )
    low, high, rows = row_blocks(width)
    n_ctx, c = lax.axis_size("ctx"), lax.axis_index("ctx")
    held = part((2 * high + low) * rows, rows) + near[1] + far
    block = rows // n_ctx
    total = lax.dynamic_slice_in_dim(held, c * block, block, 0)
    for k in range(1, n_ctx):
        give = lax.dynamic_slice_in_dim(held, lax.rem(c + k, n_ctx) * block, block, 0)
        total = total + lax.ppermute(give, "ctx", [(m, (m + k) % n_ctx) for m in range(n_ctx)])
    return total


def tie(first, second):
    return lax.optimization_barrier((first, second))


def chain(own, totals, backward):
    count = lax.axis_size("ctx")
    if count == 1:
        return [jnp.zeros_like(part) for part in own]
    received = entering = list(own)
    for hop in range(count - 1):
        pair = (count - 1 - hop, count - 2 - hop) if backward else (hop, hop + 1)
        leaving = own if hop == 0 else [t * r + o for t, r, o in zip(totals, received, own)]
        received = []
        for part in leaving:
            received.append(lax.ppermute(part, "ctx", [pair]))
        entering = received if hop == 0 else [e + r for e, r in zip(entering, received)]
    return entering


def segment_lengths():
    return [CONV * INNER, INNER, INNER, 2 * CONV * STATE, 2 * STATE, HEADS, HEADS, HEADS, D]


def unpack(flat):
    pieces = []
    offset = 0
    for length in segment_lengths():
        pieces.append(flat[offset : offset + length])
        offset += length
    return pieces


def silu_grad(value):
    sigma = jax.nn.sigmoid(value)
    return sigma * (1.0 + value * (1.0 - sigma))


def conv_forward(extended, kernel, offset_bias, length):
    total = jnp.zeros(extended[:, :length].shape, F32) + offset_bias
    for tap_index in range(CONV):
        total = total + kernel[tap_index] * extended[:, tap_index : tap_index + length]
    return total


def conv_backward(slope, follow, extended, kernel, length):
    padded = jnp.concatenate([slope, follow], axis=1)
    grad_input = jnp.zeros(slope.shape, F32)
    kernel_grads = []
    for tap_index in range(CONV):
        begin = CONV - 1 - tap_index
        grad_input = grad_input + kernel[tap_index] * padded[:, begin : begin + length]
        kernel_grads.append(
            jnp.sum(slope * extended[:, tap_index : tap_index + length], axis=(0, 1))
        )
    return (grad_input, jnp.stack(kernel_grads), jnp.sum(slope, axis=(0, 1)))


def dot(left, right, contract, exact=False):
    return lax.dot_general(
        left,
        right,
        ((contract[:1], contract[1:]), ((), ())),
        precision=HIGH if exact else None,
        preferred_element_type=F32,
    )


def adam_update(weight, moment, second, gradient, rate):
    moment = BETA_ONE * moment + (1.0 - BETA_ONE) * gradient
    second = BETA_TWO * second + (1.0 - BETA_TWO) * gradient * gradient
    moment_hat = moment / (1.0 - BETA_ONE**STEP)
    second_hat = second / (1.0 - BETA_TWO**STEP)
    weight = weight - rate * (moment_hat / (jnp.sqrt(second_hat) + ADAM_EPS) + DECAY_RATE * weight)
    return (weight, moment, second)


def einsum(spec, *parts):
    return jnp.einsum(spec, *parts, precision=HIGH, preferred_element_type=F32)


def on_device(
    layer_input,
    cotangent,
    in_proj,
    delta_proj,
    out_proj,
    state_proj,
    packed_params,
    moment_in,
    moment_delta,
    moment_out,
    moment_state,
    moment_packed,
    square_in,
    square_delta,
    square_out,
    square_state,
    square_packed,
):
    sizes = (lax.axis_size("dp"), lax.axis_size("ctx"), lax.axis_size("tensor"))
    n_dp, n_ctx, n_t = sizes
    groups = n_dp * n_ctx
    rank = lax.axis_index("tensor")
    seqs, tokens, width = layer_input.shape
    rows = seqs * tokens
    local_inner = in_proj.shape[2]
    local_heads = delta_proj.shape[1]
    own_width = width // n_t
    rim = CONV - 1

    state_rows_own = state_proj.shape[0]
    pack_own = packed_params.shape[0]
    state_piece = jnp.concatenate(
        [state_proj[:, 0].astype(BF), state_proj[:, 1].astype(BF)], axis=0
    )
    state_pad = cdiv(2 * state_rows_own, 16) * 16
    delta_pad = cdiv(local_heads, 16) * 16
    pack_rows = cdiv(pack_own, LANES)
    pack_pad = cdiv(pack_rows, 16) * 16
    proj_rows = delta_proj.shape[0]
    block = jnp.concatenate(
        [
            jnp.pad(state_piece, ((0, state_pad - 2 * state_rows_own), (0, 0))),
            jnp.pad(
                delta_proj.astype(BF).T, ((0, delta_pad - local_heads), (0, LANES - proj_rows))
            ),
            jnp.pad(
                jnp.pad(packed_params.astype(BF), (0, pack_rows * LANES - pack_own)).reshape(
                    pack_rows, LANES
                ),
                ((0, pack_pad - pack_rows), (0, 0)),
            ),
        ],
        axis=0,
    )
    small = gather_small(block, sizes)
    wx = lax.all_gather(in_proj[:, 1].astype(BF), ("dp", "ctx"), axis=0, tiled=True)
    wz = lax.all_gather(in_proj[:, 0].astype(BF), ("dp", "ctx"), axis=0, tiled=True)
    wo = lax.all_gather(out_proj.astype(BF), ("dp", "ctx"), axis=0, tiled=True)
    up_own = cotangent.astype(BF)
    if n_t == 2:
        up_away = swap(up_own)
        first = rank == 0
        up_full = jnp.concatenate(
            [jnp.where(first, up_own, up_away), jnp.where(first, up_away, up_own)], axis=2
        )
    else:
        up_full = lax.all_gather(up_own, "tensor", axis=2, tiled=True)
    up_rows = up_full.reshape(rows, width)

    state_slots = small[..., : 2 * state_rows_own, :].reshape(-1, 2, state_rows_own, STATE)
    ws = jnp.concatenate(
        [state_slots[:, 0].reshape(width, STATE), state_slots[:, 1].reshape(width, STATE)], axis=1
    )
    delta_slots = lax.dynamic_index_in_dim(small, rank, 2, False)
    delta_slots = delta_slots[..., state_pad : state_pad + local_heads, :proj_rows]
    wd = delta_slots.reshape(groups, local_heads, proj_rows).transpose(0, 2, 1)
    wd = wd.reshape(width, local_heads)
    pack_slots = small[..., state_pad + delta_pad : state_pad + delta_pad + pack_rows, :]
    packed = pack_slots.reshape(groups * n_t, pack_rows * LANES)[:, :pack_own].reshape(-1)
    pieces = unpack(packed.astype(F32))
    conv_kernel = lax.dynamic_slice_in_dim(
        pieces[0].reshape(CONV, INNER), rank * local_inner, local_inner, 1
    )
    conv_bias = lax.dynamic_slice_in_dim(pieces[1], rank * local_inner, local_inner, 0)
    gate_gain = lax.dynamic_slice_in_dim(pieces[2], rank * local_inner, local_inner, 0)
    state_kernel = pieces[3].reshape(CONV, 2 * STATE)
    state_bias = pieces[4]
    delta_bias = lax.dynamic_slice_in_dim(pieces[5], rank * local_heads, local_heads, 0)
    log_rates = lax.dynamic_slice_in_dim(pieces[6], rank * local_heads, local_heads, 0)
    skip_gain = lax.dynamic_slice_in_dim(pieces[7], rank * local_heads, local_heads, 0)
    norm_gain = pieces[8]
    rates = -jnp.exp(log_rates)

    input_float = layer_input.astype(F32)
    inverse = lax.rsqrt(jnp.mean(input_float * input_float, axis=-1, keepdims=True) + NORM_EPS)
    normed = (input_float * inverse * norm_gain).astype(BF).reshape(rows, width)
    sproj = dot(normed, ws, (1, 0)).astype(BF).reshape(seqs, tokens, 2 * STATE)
    raw = dot(normed, wd, (1, 0)).reshape(seqs, tokens, local_heads)
    xproj = dot(normed, wx, (1, 0)).astype(BF).reshape(seqs, tokens, local_inner)
    tails = from_behind(
        jnp.concatenate([xproj[:, tokens - rim :], sproj[:, tokens - rim :]], axis=2), "ctx", 1
    )
    ext_x = jnp.concatenate([tails[:, :, :local_inner], xproj], axis=1).astype(F32)
    ext_s = jnp.concatenate([tails[:, :, local_inner:], sproj], axis=1).astype(F32)
    conv_x = conv_forward(ext_x, conv_kernel, conv_bias, tokens)
    conv_s = conv_forward(ext_s, state_kernel, state_bias, tokens)
    act_x = jax.nn.silu(conv_x).astype(BF)
    act_s = jax.nn.silu(conv_s).astype(BF)
    delta = jax.nn.softplus(raw + delta_bias)
    wv = act_s[:, :, :STATE]
    rv = act_s[:, :, STATE:]
    past = (jnp.arange(tokens)[:, None] >= jnp.arange(tokens)[None, :]).astype(F32)
    cum = einsum("tm,smh->sth", past, delta * rates)
    totals = jnp.exp(cum[:, -1])
    fade_decay = jnp.exp(cum[:, -1:] - cum)
    fading = fade_decay * delta
    growth = jnp.exp(cum)
    spread = [
        jnp.broadcast_to(
            jnp.repeat(totals[k], HEAD_DIM)[:, None], (local_inner, STATE)
        )
        for k in range(seqs)
    ]
    cum_t = jnp.swapaxes(cum, 1, 2)
    skip_lanes = jnp.repeat(skip_gain, HEAD_DIM)[None, :]
    own_state = [scan_state(act_x, wv, fading, k) for k in range(seqs)]
    within = scan_within(act_x, wv, rv, cum, cum_t, jnp.swapaxes(delta, 1, 2))
    own_state, normed_late = tie(own_state, normed)
    zproj = dot(normed_late, wz, (1, 0)).astype(BF).reshape(seqs, tokens, local_inner)
    entering = chain(own_state, spread, False)
    entering = jnp.stack(entering, axis=0)

    plain, mixed, square_sums = scan_gate(within, act_x, zproj, rv, growth, entering, skip_lanes)
    gate_input = zproj.astype(F32)
    gate_act = jax.nn.silu(gate_input)
    mixer = plain + skip_lanes * act_x.astype(F32)
    square_sums = sum_tensor(square_sums[:, :, 0])
    gate_inverse = lax.rsqrt(square_sums / INNER + NORM_EPS)[:, :, None]
    gated = (mixed * gate_inverse * gate_gain).astype(BF).reshape(rows, local_inner)

    def out_columns(start):
        return dot(gated, lax.dynamic_slice_in_dim(wo, start, own_width, 0), (1, 1))

    branch, branch_away = scatter_tensor(out_columns, own_width, rank)
    own_input = lax.dynamic_slice_in_dim(layer_input, rank * own_width, own_width, 2).astype(F32)

    gated_grad = dot(up_rows, wo, (1, 0)).reshape(seqs, tokens, local_inner)
    part_out = cut_dot(up_rows, gated)
    near_out = scatter_start(part_out, width)
    scaled = gated_grad * gate_gain
    row_sums = sum_tensor(jnp.sum(scaled * mixed, axis=-1))
    mixed_grad = gate_inverse * scaled - mixed * gate_inverse**3 * (row_sums / INNER)[:, :, None]
    grad_gate_gain = jnp.sum(gated_grad * mixed * gate_inverse, axis=(0, 1))
    mixer_grad = mixed_grad * gate_act
    z_grad = (mixed_grad * mixer * silu_grad(gate_input)).astype(BF).reshape(rows, local_inner)
    part_z = cut_dot(normed, z_grad)

    pulled = [scan_state(mixer_grad, rv, growth, k) for k in range(seqs)]
    dy = mixer_grad
    dx_bare, dw, dr = scan_within_back(dy, act_x, wv, rv, cum, cum_t, delta)
    dx_bare, near_out = tie(dx_bare, near_out)
    far_out = scatter_high(part_out, width, near_out)
    near_z = scatter_start(part_z, width)
    leaving = jnp.stack(chain(pulled, spread, True), axis=0)
    leaving, (far_out, near_z) = tie(leaving, (far_out, near_z))
    far_z = scatter_high(part_z, width, near_z)
    grad_out = scatter_end(part_out, width, near_out, far_out)
    dx, dw, dr, bare_dot, fade_dot, plain_dot, skip_dot = scan_state_back(
        dy, act_x, plain, dx_bare, wv, delta, fading, growth, entering, leaving, skip_lanes, dw, dr
    )
    cum_grad = plain_dot - delta * bare_dot - fading * fade_dot
    end_grad = jnp.sum(fading * fade_dot, axis=1) + totals * jnp.sum(
        (leaving * entering).reshape(seqs, local_heads, HEAD_DIM, STATE), axis=(2, 3)
    )
    step_grad = (
        einsum("tm,sth->smh", past, cum_grad) + end_grad[:, None, :]
    )
    delta_grad = bare_dot + fade_decay * fade_dot + rates * step_grad
    grad_rates = jnp.sum(delta * step_grad, axis=(0, 1))
    grad_skip = jnp.sum(skip_dot.reshape(seqs, local_heads, HEAD_DIM), axis=(0, 2))
    grad_log_rates = grad_rates * rates
    raw_grad = delta_grad * jax.nn.sigmoid(raw + delta_bias)
    grad_delta_bias = jnp.sum(raw_grad, axis=(0, 1))

    slope_x = dx.reshape(seqs, tokens, local_inner) * silu_grad(conv_x)
    slope_s = jnp.concatenate([dw, dr], axis=-1) * silu_grad(conv_s)
    follow = from_behind(
        jnp.concatenate([slope_x[:, :rim], slope_s[:, :rim]], axis=2), "ctx", -1
    )
    back_x, grad_conv_kernel, grad_conv_bias = conv_backward(
        slope_x, follow[:, :, :local_inner], ext_x, conv_kernel, tokens
    )
    back_s, grad_state_kernel, grad_state_bias = conv_backward(
        slope_s, follow[:, :, local_inner:], ext_s, state_kernel, tokens
    )
    x_grad = back_x.astype(BF).reshape(rows, local_inner)
    state_rows = back_s.reshape(rows, 2 * STATE)
    raw_rows = raw_grad.reshape(rows, local_heads)

    def normed_columns(start):
        def cut(weight):
            return lax.dynamic_slice_in_dim(weight, start, own_width, 0)

        product = dot(x_grad, cut(wx), (1, 1))
        return (
            product
            + dot(z_grad, cut(wz), (1, 1))
            + dot(state_rows, cut(ws).astype(F32), (1, 1), True)
            + dot(raw_rows, cut(wd).astype(F32), (1, 1), True)
        )

    x_grad, (branch_away, far_z, grad_out) = tie(x_grad, (branch_away, far_z, grad_out))
    layer_output = own_input + (branch + branch_away).reshape(seqs, tokens, own_width)
    grad_z = scatter_end(part_z, width, near_z, far_z)
    pieces_x = 3 if local_inner % (3 * LANES) == 0 else 1
    piece = local_inner // pieces_x
    parts_x = [
        cut_dot(normed, x_grad[:, k * piece : (k + 1) * piece]) for k in range(pieces_x)
    ]
    near_x = []
    for part in parts_x:
        near_x.append(scatter_start(part, width))

    starts = [(1 - rank) * own_width, rank * own_width]
    if n_t != 2:
        starts = [k * own_width for k in range(n_t)]
    columns = [normed_columns(start) for start in starts]
    if n_t == 2:
        normed_grad = columns[1] + swap(columns[0])
    else:
        normed_grad = lax.psum_scatter(
            jnp.concatenate(columns, axis=1), "tensor", scatter_dimension=1, tiled=True
        )
    normed_grad = normed_grad.reshape(seqs, tokens, own_width)
    own_gain = lax.dynamic_slice_in_dim(norm_gain, rank * own_width, own_width, 0)
    grad_norm_gain = jnp.zeros((D,), F32)
    in_sums = 0.0
    for start, part in zip(starts, columns):
        inputs = lax.dynamic_slice_in_dim(layer_input, start, own_width, 2).astype(F32)
        gain = lax.dynamic_slice_in_dim(norm_gain, start, own_width, 0)
        product = part.reshape(seqs, tokens, own_width) * inputs
        in_sums = in_sums + jnp.sum(product * gain, axis=-1)
        grad_norm_gain = lax.dynamic_update_slice_in_dim(
            grad_norm_gain, jnp.sum(product * inverse, axis=(0, 1)), start, 0
        )
    in_mean = sum_tensor(in_sums)[:, :, None] / width
    scaled_in = normed_grad * own_gain
    input_grad = cotangent + inverse * scaled_in - own_input * inverse**3 * in_mean

    normed_float = normed.astype(F32)
    grad_state_part = dot(normed_float, state_rows, (0, 0), True)
    grad_delta_part = dot(normed_float, raw_rows, (0, 0), True)

    def widen(local_values, full_length):
        return lax.dynamic_update_slice_in_dim(
            jnp.zeros((full_length,), F32), local_values, rank * local_values.shape[0], 0
        )

    conv_wide = lax.dynamic_update_slice_in_dim(
        jnp.zeros((CONV, INNER), F32), grad_conv_kernel, rank * local_inner, 1
    ).reshape(-1)
    joined = jnp.concatenate(
        [
            conv_wide,
            widen(grad_conv_bias, INNER),
            widen(grad_gate_gain, INNER),
            grad_state_kernel.reshape(-1),
            grad_state_bias,
            widen(grad_delta_bias, HEADS),
            widen(grad_log_rates, HEADS),
            widen(grad_skip, HEADS),
            grad_norm_gain,
        ]
    )
    pack_group = n_t * pack_own
    packed_part = jnp.pad(joined, (0, groups * pack_group - joined.shape[0]))
    pack_cols = cdiv(pack_group, proj_rows)
    packed_part = jnp.pad(
        packed_part.reshape(groups, pack_group), ((0, 0), (0, pack_cols * proj_rows - pack_group))
    ).reshape(width, pack_cols)
    extra_pad = cdiv(local_heads + pack_cols, LANES) * LANES - local_heads - pack_cols
    tail_part = jnp.concatenate(
        [
            grad_state_part,
            grad_delta_part,
            packed_part,
            jnp.zeros((width, extra_pad), F32),
        ],
        axis=1,
    )
    far_x = [scatter_high(part, width, near) for part, near in zip(parts_x, near_x)]
    grad_x = jnp.concatenate(
        [
            scatter_end(part, width, near, far)
            for part, near, far in zip(parts_x, near_x, far_x)
        ],
        axis=1,
    )

    def part_tail(start, rows):
        return lax.dynamic_slice_in_dim(tail_part, start, rows, 0)

    near_tail = scatter_start(part_tail, width)
    far_tail = scatter_high(part_tail, width, near_tail)
    tail = scatter_end(part_tail, width, near_tail, far_tail)
    at = 2 * STATE
    grad_delta = tail[:, at : at + local_heads]
    state_group = tail[:, :at]
    packed_group = tail[:, at + local_heads : at + local_heads + pack_cols]
    packed_group = packed_group.reshape(-1)[:pack_group]
    if n_t == 2:
        away = swap(
            (
                lax.dynamic_slice_in_dim(
                    state_group, (1 - rank) * state_rows_own, state_rows_own, 0
                ),
                lax.dynamic_slice_in_dim(packed_group, (1 - rank) * pack_own, pack_own, 0),
            )
        )
        grad_state = (
            lax.dynamic_slice_in_dim(state_group, rank * state_rows_own, state_rows_own, 0)
            + away[0]
        )
        grad_packed = (
            lax.dynamic_slice_in_dim(packed_group, rank * pack_own, pack_own, 0) + away[1]
        )
    else:
        grad_state = lax.psum_scatter(state_group, "tensor", scatter_dimension=0, tiled=True)
        grad_packed = lax.psum_scatter(packed_group, "tensor", scatter_dimension=0, tiled=True)
    grad_state = grad_state.reshape(state_rows_own, 2, STATE)
    grad_in = jnp.stack([grad_z, grad_x], axis=1)

    new_in, next_moment_in, next_square_in = adam_update(
        in_proj, moment_in, square_in, grad_in, MATRIX_RATE
    )
    new_delta, next_moment_delta, next_square_delta = adam_update(
        delta_proj, moment_delta, square_delta, grad_delta, MATRIX_RATE
    )
    new_out, next_moment_out, next_square_out = adam_update(
        out_proj, moment_out, square_out, grad_out, MATRIX_RATE
    )
    new_state, next_moment_state, next_square_state = adam_update(
        state_proj, moment_state, square_state, grad_state, MATRIX_RATE
    )
    new_packed, next_moment_packed, next_square_packed = adam_update(
        packed_params, moment_packed, square_packed, grad_packed, PACKED_RATE
    )
    return (
        layer_output,
        input_grad,
        grad_in,
        grad_delta,
        grad_out,
        grad_state,
        grad_packed,
        new_in,
        new_delta,
        new_out,
        new_state,
        new_packed,
        next_moment_in,
        next_moment_delta,
        next_moment_out,
        next_moment_state,
        next_moment_packed,
        next_square_in,
        next_square_delta,
        next_square_out,
        next_square_state,
        next_square_packed,
    )


def solution(mesh):
    matrix = P(("dp", "ctx"), "tensor")
    projection = P(("dp", "ctx"), None, "tensor")
    state = P(("dp", "ctx", "tensor"), None, None)
    flat = P(("dp", "ctx", "tensor"))
    tokens = P("dp", "ctx", "tensor")
    weights = (projection, matrix, matrix, state, flat)

    return jax.shard_map(
        on_device,
        mesh=mesh,
        in_specs=(P("dp", "ctx", None), tokens) + weights * 3,
        out_specs=(tokens, tokens) + weights * 4,
        check_vma=False,
    )
```

profile of v0, /device:TPU:0, one launch (start us, length us, event | category | flops | bytes accessed | tf_op | source)
XLA Modules:
  0.0 857.0 jit_solution(16894668458544004594)
XLA Ops:
  16.2 51.0 %gather_small.1 = bf16[4,4,2,144,128]{4,3,2,1,0:T(8,128)(2,1)} custom-call(bf16[144,128]{1,0:T(8,128)(2,1)} %fusion.148.in_ref), custom_call_target="tpu_custom_call" | custom-call | tf_op jit(solution)/shard_map/gather_small/pallas_call | solution.py:111
  144.6 15.5 %shard_map.336.within_ref = f32[3,256,1536]{2,1,0:T(8,128)} custom-call(bf16[3,256,1536]{2,1,0:T(8,128)(2,1)} %get-tuple-element.213.x_ref.v_ref, bf16[3,256,128]{2,1,0:T(8,128)(2,1)} %get-tuple-element.251.w_ref.u_ref, bf16[3,256,128]{2,1,0:T(8,128)(2,1)} %get-tuple-element.250.r_ref.u_ref, f32[3,256,24]{2,1,0:T(8,128)} %bitcast.243, ...), custom_call_target="tpu_custom_call" | custom-call | flops 4831838208 | bytes 7077888 | tf_op jit(solution)/shard_map/pallas_call | solution.py:395
  162.4 24.4 %collective-permute-done.4 = f32[1536,128]{1,0:T(8,128)} collective-permute-done((f32[1536,128]{1,0:T(8,128)}, f32[1536,128]{1,0:T(8,128)}, u32[]{:S(2)}, u32[]{:S(2)}) %collective-permute-start.4) | collective-permute-done | bytes 786464 | tf_op jit(solution)/shard_map/ppermute | solution.py:536
  188.9 22.3 %collective-permute-done.7 = f32[1536,128]{1,0:T(8,128)} collective-permute-done((f32[1536,128]{1,0:T(8,128)}, f32[1536,128]{1,0:T(8,128)}, u32[]{:S(2)}, u32[]{:S(2)}) %collective-permute-start.7) | collective-permute-done | bytes 786464 | tf_op jit(solution)/shard_map/ppermute | solution.py:536
  222.4 13.7 %shard_map.340 = (f32[3,256,1536]{2,1,0:T(8,128)}, f32[3,256,1536]{2,1,0:T(8,128)}, f32[3,256,1]{2,1,0:T(8,128)}) custom-call(f32[3,256,1536]{2,1,0:T(8,128)} %shard_map.336.within_ref, bf16[3,256,1536]{2,1,0:T(8,128)(2,1)} %get-tuple-element.213.x_ref.v_ref, bf16[3,256,1536]{2,1,0:T(8,128)(2,1)} %bitcast.224, ...), custom_call_target="tpu_custom_call" | custom-call | flops 1207959552 | bytes 18874368 | tf_op jit(solution)/shard_map/pallas_call | solution.py:407
  241.7 10.7 %multiply_reduce_fusion = (f32[1536]{0:T(1024)S(1)}, f32[3,256]{1,0:T(4,128)S(1)}, f32[3,256,1536]{2,1,0:T(8,128)}) fusion(f32[3,256,1536]{2,1,0:T(8,128)} %get-tuple-element.54, f32[3,256]{1,0:T(4,128)S(1)} %get-tuple-element.210, f32[1536]{0:T(1024)S(1)} %dynamic_slice.205, bf16[1536,1536]{1,0:T(8,128)(2,1)} %all-gather.6.cloned.1.call-done, ...), kind=kOutput, calls=%fused_computation.34 | convolution fusion | flops 3635672832 | bytes 16533504 | tf_op jit(solution)/shard_map/dot_general | solution.py:580
  256.0 10.1 %fusion.18 = (bf16[3,256,1536]{2,1,0:T(8,128)(2,1)}, f32[3,256,1536]{2,1,0:T(8,128)}, bf16[3,256,1536]{2,1,0:T(8,128)(2,1)}) fusion(bf16[3,256,1536]{2,1,0:T(8,128)(2,1)} %bitcast.225, f32[3,256,1536]{2,1,0:T(8,128)} %get-tuple-element.56.plain_ref, bf16[3,256,1536]{2,1,0:T(8,128)(2,1)S(1)} %copy-done.1, f32[1536]{0:T(1024)S(1)} %mul.771, ...), kind=kLoop, calls=%fused_computation.25 | loop fusion | flops 28311552 | bytes 28333056 | tf_op jit(solution)/shard_map/convert_element_type | solution.py:757
  294.0 24.9 %shard_map.341 = (f32[3,256,1536]{2,1,0:T(8,128)}, f32[3,256,128]{2,1,0:T(8,128)}, f32[3,256,128]{2,1,0:T(8,128)}) custom-call(f32[3,256,1536]{2,1,0:T(8,128)} %get-tuple-element.216.dy_ref.v_ref, bf16[3,256,1536]{2,1,0:T(8,128)(2,1)} %get-tuple-element.213.x_ref.v_ref, bf16[3,256,128]{2,1,0:T(8,128)(2,1)} %get-tuple-element.251.w_ref.u_ref, ...), custom_call_target="tpu_custom_call" | custom-call | flops 9663676416 | bytes 11796480 | tf_op jit(solution)/shard_map/pallas_call | solution.py:422
  353.0 97.1 %collective-permute-done.17 = f32[1536,128]{1,0:T(8,128)S(1)} collective-permute-done((f32[1536,128]{1,0:T(8,128)S(1)}, f32[1536,128]{1,0:T(8,128)S(1)}, u32[]{:S(2)}, u32[]{:S(2)}) %collective-permute-start.17) | collective-permute-done | bytes 786464 | tf_op jit(solution)/shard_map/ppermute | solution.py:536
  451.6 15.4 %collective-permute-done.20 = f32[1536,128]{1,0:T(8,128)S(1)} collective-permute-done((f32[1536,128]{1,0:T(8,128)S(1)}, f32[1536,128]{1,0:T(8,128)S(1)}, u32[]{:S(2)}, u32[]{:S(2)}) %collective-permute-start.20) | collective-permute-done | bytes 786464 | tf_op jit(solution)/shard_map/ppermute | solution.py:536
  467.9 14.0 %collective-permute-done.23 = f32[1536,128]{1,0:T(8,128)S(1)} collective-permute-done((f32[1536,128]{1,0:T(8,128)S(1)}, f32[1536,128]{1,0:T(8,128)S(1)}, u32[]{:S(2)}, u32[]{:S(2)}) %collective-permute-start.23) | collective-permute-done | bytes 786464 | tf_op jit(solution)/shard_map/ppermute | solution.py:536
  485.3 22.0 %shard_map.345 = (f32[3,256,1536]{2,1,0:T(8,128)}, f32[3,256,128]{2,1,0:T(8,128)}, f32[3,256,128]{2,1,0:T(8,128)}, f32[3,256,24]{2,1,0:T(8,128)}, f32[3,256,24]{...) custom-call(f32[3,256,1536]{2,1,0:T(8,128)} %get-tuple-element.216.dy_ref.v_ref, ...), custom_call_target="tpu_custom_call" | custom-call | flops 3623878656 | bytes 25952256 | tf_op jit(solution)/shard_map/pallas_call | solution.py:436
  523.1 15.6 %collective-permute-start.30 = (f32[96,1536]{1,0:T(8,128)}, f32[96,1536]{1,0:T(8,128)}, u32[]{:S(2)}, u32[]{:S(2)}) collective-permute-start(f32[96,1536]{1,0:T(8,128)} %get-tuple-element.225), channel_id=1, source_target_pairs={{0,2},{2,4},{4,6},{6,0},{1,3},{3,5},{5,7},{7,1},{8,10},{10,12},{12... | collective-permute-start | bytes 1769480 | tf_op jit(solution)/shard_map/ppermute | solution.py:518
  556.7 9.0 %collective-permute-done.27 = f32[3,3,1792]{2,1,0:T(4,128)S(1)} collective-permute-done((f32[3,3,1792]{2,1,0:T(4,128)S(1)}, f32[3,3,1792]{2,1,0:T(4,128)S(1)}, u32[]{:S(2)}, u32[]{:S(2)}) %collective-permute-start.27) | collective-permute-done | bytes 64544 | tf_op jit(solution)/shard_map/ppermute | solution.py:449
  585.3 33.5 %collective-permute-done.29 = f32[384,1536]{1,0:T(8,128)S(1)} collective-permute-done((f32[384,1536]{1,0:T(8,128)}, f32[384,1536]{1,0:T(8,128)S(1)}, u32[]{:S(2)}, u32[]{:S(2)}) %collective-permute-start.29) | collective-permute-done | bytes 2359328 | tf_op jit(solution)/shard_map/ppermute | solution.py:471
  651.9 13.9 %collective-permute-start.35 = (f32[96,1536]{1,0:T(8,128)S(1)}, f32[96,1536]{1,0:T(8,128)S(1)}, u32[]{:S(2)}, u32[]{:S(2)}) collective-permute-start(f32[96,1536]{1,0:T(8,128)S(1)} %get-tuple-element.220), channel_id=1, source_target_pairs={{0,2},{2,4},{4,6},{6,0},{1,3},{3,5},{5,7},{7,1},{8,10},{10,12},{12... | collective-permute-start | bytes 1769480 | tf_op jit(solution)/shard_map/ppermute | solution.py:518
  679.5 14.1 %collective-permute-done.36 = f32[96,1536]{1,0:T(8,128)S(1)} collective-permute-done((f32[96,1536]{1,0:T(8,128)S(1)}, f32[96,1536]{1,0:T(8,128)S(1)}, u32[]{:S(2)}, u32[]{:S(2)}) %collective-permute-start.36) | collective-permute-done | bytes 589856 | tf_op jit(solution)/shard_map/ppermute | solution.py:518
  693.6 9.5 %collective-permute-done.37 = f32[96,1536]{1,0:T(8,128)S(1)} collective-permute-done((f32[96,1536]{1,0:T(8,128)S(1)}, f32[96,1536]{1,0:T(8,128)S(1)}, u32[]{:S(2)}, u32[]{:S(2)}) %collective-permute-start.37) | collective-permute-done | bytes 589856 | tf_op jit(solution)/shard_map/ppermute | solution.py:518
  707.3 9.4 %collective-permute-done.58 = f32[384,384]{0,1:T(8,128)S(1)} collective-permute-done((f32[384,384]{0,1:T(8,128)S(1)}, f32[384,384]{0,1:T(8,128)S(1)}, u32[]{:S(2)}, u32[]{:S(2)}) %collective-permute-start.58) | collective-permute-done | bytes 589856 | tf_op jit(solution)/shard_map/ppermute | solution.py:471
  717.2 15.0 %collective-permute-start.59 = (f32[96,384]{0,1:T(8,128)S(1)}, f32[96,384]{0,1:T(8,128)S(1)}, u32[]{:S(2)}, u32[]{:S(2)}) collective-permute-start(f32[96,384]{0,1:T(8,128)S(1)} %get-tuple-element.242), channel_id=1, source_target_pairs={{0,2},{2,4},{4,6},{6,0},{1,3},{3,5},{5,7},{7,1},{8,10},{10,12},{12... | collective-permute-start | bytes 442376 | tf_op jit(solution)/shard_map/ppermute | solution.py:518
  760.4 8.6 collective-permute-done.40
  772.8 13.0 %collective-permute-done.46 = f32[384,512]{1,0:T(8,128)} collective-permute-done((f32[384,512]{1,0:T(8,128)}, f32[384,512]{1,0:T(8,128)}, u32[]{:S(2)}, u32[]{:S(2)}) %collective-permute-start.46) | collective-permute-done | bytes 786464 | tf_op jit(solution)/shard_map/ppermute | solution.py:471
  791.5 10.0 %collective-permute-done.52 = f32[384,512]{1,0:T(8,128)S(1)} collective-permute-done((f32[384,512]{1,0:T(8,128)}, f32[384,512]{1,0:T(8,128)S(1)}, u32[]{:S(2)}, u32[]{:S(2)}) %collective-permute-start.52) | collective-permute-done | bytes 786464 | tf_op jit(solution)/shard_map/ppermute | solution.py:471
  823.8 10.7 %collective-permute-done.54 = f32[96,512]{1,0:T(8,128)S(1)} collective-permute-done((f32[96,512]{1,0:T(8,128)S(1)}, f32[96,512]{1,0:T(8,128)S(1)}, u32[]{:S(2)}, u32[]{:S(2)}) %collective-permute-start.54) | collective-permute-done | bytes 196640 | tf_op jit(solution)/shard_map/ppermute | solution.py:518
  (587 shorter events, 357.2 us)
Async XLA Ops:
  7.2 81.0 %all-gather.8.cloned.1.call-start = ((), (), s32[]{:S(2)}) async-start(), calls=%async_computation.1 | async-start | bytes 5013504 | tf_op jit(solution)/shard_map/all_gather | solution.py:658
  9.7 127.3 %all-gather.10.cloned.1.call-start = ((), (), s32[]{:S(2)}) async-start(), calls=%async_computation.2 | async-start | bytes 5013504 | tf_op jit(solution)/shard_map/all_gather | solution.py:659
  10.5 231.2 %all-gather.6.cloned.1.call-start = ((), (), s32[]{:S(2)}) async-start(), calls=%async_computation | async-start | bytes 5013504 | tf_op jit(solution)/shard_map/all_gather | solution.py:660
  11.7 227.1 %collective-permute-start.11 = (bf16[3,256,768]{2,1,0:T(8,128)(2,1)}, bf16[3,256,768]{2,1,0:T(8,128)(2,1)}, u32[]{:S(2)}, u32[]{:S(2)}) collective-permute-start(bf16[3,256,768]{2,1,0:T(8,128)(2,1)} %convert_element_type.119), channel_id=1, source_target_pairs={{0,1},{1,0},{2,3},{3,2},{4,5},{5,4},{6,7},{7,6},{8,9},{9,8},{10,11... | collective-permute-start | bytes 3538952 | tf_op jit(solution)/shard_map/ppermute | solution.py:453
  132.5 54.3 %collective-permute-start.4 = (f32[1536,128]{1,0:T(8,128)}, f32[1536,128]{1,0:T(8,128)}, u32[]{:S(2)}, u32[]{:S(2)}) collective-permute-start(f32[1536,128]{1,0:T(8,128)} %shard_map.338), channel_id=1, source_target_pairs={{0,2},{1,3},{8,10},{9,11},{16,18},{17,19},{24,26},{25,27}} | collective-permute-start | bytes 2359304 | tf_op jit(solution)/shard_map/ppermute | solution.py:536
  134.7 76.5 %collective-permute-start.7 = (f32[1536,128]{1,0:T(8,128)}, f32[1536,128]{1,0:T(8,128)}, u32[]{:S(2)}, u32[]{:S(2)}) collective-permute-start(f32[1536,128]{1,0:T(8,128)} %shard_map.339), channel_id=1, source_target_pairs={{0,2},{1,3},{8,10},{9,11},{16,18},{17,19},{24,26},{25,27}} | collective-permute-start | bytes 2359304 | tf_op jit(solution)/shard_map/ppermute | solution.py:536
  161.7 51.7 %collective-permute-start.2 = (f32[1536,128]{1,0:T(8,128)S(1)}, f32[1536,128]{1,0:T(8,128)S(1)}, u32[]{:S(2)}, u32[]{:S(2)}) collective-permute-start(f32[1536,128]{1,0:T(8,128)S(1)} %multiply_add_fusion.12), channel_id=1, source_target_pairs={{2,4},{3,5},{10,12},{11,13},{18,20},{19,21},{26,28},{27,29}} | collective-permute-start | bytes 2359304 | tf_op jit(solution)/shard_map/ppermute | solution.py:536
  293.4 51.5 %collective-permute-start.14 = (f32[384,1536]{1,0:T(8,128)}, f32[384,1536]{1,0:T(8,128)}, u32[]{:S(2)}, u32[]{:S(2)}) collective-permute-start(f32[384,1536]{1,0:T(8,128)} %fusion.76), channel_id=1, source_target_pairs={{0,8},{8,0},{16,24},{24,16},{1,9},{9,1},{17,25},{25,17},{2,10},{10... | collective-permute-start | bytes 7077896 | tf_op jit(solution)/shard_map/ppermute | solution.py:471
  293.5 52.8 %collective-permute-start.13 = (f32[384,1536]{1,0:T(8,128)}, f32[384,1536]{1,0:T(8,128)}, u32[]{:S(2)}, u32[]{:S(2)}) collective-permute-start(f32[384,1536]{1,0:T(8,128)} %fusion.78), channel_id=1, source_target_pairs={{0,8},{8,0},{16,24},{24,16},{1,9},{9,1},{17,25},{25,17},{2,10},{10... | collective-permute-start | bytes 7077896 | tf_op jit(solution)/shard_map/ppermute | solution.py:471
  340.6 141.6 %collective-permute-start.25 = (f32[384,1536]{1,0:T(8,128)S(1)}, f32[384,1536]{1,0:T(8,128)}, u32[]{:S(2)}, u32[]{:S(2)}) collective-permute-start(f32[384,1536]{1,0:T(8,128)S(1)} %copy-done.57), channel_id=1, source_target_pairs={{0,8},{8,0},{16,24},{24,16},{1,9},{9,1},{17,25},{25,17},{2,10},{10... | collective-permute-start | bytes 7077896 | tf_op jit(solution)/shard_map/ppermute | solution.py:471
  343.2 139.1 %collective-permute-start.26 = (f32[384,1536]{1,0:T(8,128)S(1)}, f32[384,1536]{1,0:T(8,128)}, u32[]{:S(2)}, u32[]{:S(2)}) collective-permute-start(f32[384,1536]{1,0:T(8,128)S(1)} %copy-done.56), channel_id=1, source_target_pairs={{0,8},{8,0},{16,24},{24,16},{1,9},{9,1},{17,25},{25,17},{2,10},{10... | collective-permute-start | bytes 7077896 | tf_op jit(solution)/shard_map/ppermute | solution.py:471
  345.0 105.2 %collective-permute-start.17 = (f32[1536,128]{1,0:T(8,128)S(1)}, f32[1536,128]{1,0:T(8,128)S(1)}, u32[]{:S(2)}, u32[]{:S(2)}) collective-permute-start(f32[1536,128]{1,0:T(8,128)S(1)} %multiply_add_fusion.5), channel_id=1, source_target_pairs={{2,0},{3,1},{10,8},{11,9},{18,16},{19,17},{26,24},{27,25}} | collective-permute-start | bytes 2359304 | tf_op jit(solution)/shard_map/ppermute | solution.py:536
  346.3 120.7 %collective-permute-start.20 = (f32[1536,128]{1,0:T(8,128)S(1)}, f32[1536,128]{1,0:T(8,128)S(1)}, u32[]{:S(2)}, u32[]{:S(2)}) collective-permute-start(f32[1536,128]{1,0:T(8,128)S(1)} %multiply_add_fusion.3), channel_id=1, source_target_pairs={{2,0},{3,1},{10,8},{11,9},{18,16},{19,17},{26,24},{27,25}} | collective-permute-start | bytes 2359304 | tf_op jit(solution)/shard_map/ppermute | solution.py:536
  350.6 131.6 %collective-permute-start.24 = (f32[384,1536]{1,0:T(8,128)S(1)}, f32[384,1536]{1,0:T(8,128)}, u32[]{:S(2)}, u32[]{:S(2)}) collective-permute-start(f32[384,1536]{1,0:T(8,128)S(1)} %fusion.73), channel_id=1, source_target_pairs={{0,16},{8,24},{16,0},{24,8},{1,17},{9,25},{17,1},{25,9},{2,18},{10... | collective-permute-start | bytes 7077896 | tf_op jit(solution)/shard_map/ppermute | solution.py:471
  467.0 118.3 %collective-permute-start.28 = (f32[768,768]{1,0:T(8,128)}, f32[768,768]{1,0:T(8,128)}, u32[]{:S(2)}, u32[]{:S(2)}) collective-permute-start(f32[768,768]{1,0:T(8,128)} %fusion.46), channel_id=1, source_target_pairs={{0,1},{1,0},{2,3},{3,2},{4,5},{5,4},{6,7},{7,6},{8,9},{9,8},{10,11... | collective-permute-start | bytes 7077896 | tf_op jit(solution)/shard_map/ppermute | solution.py:453
  523.1 59.6 %collective-permute-start.30 = (f32[96,1536]{1,0:T(8,128)}, f32[96,1536]{1,0:T(8,128)}, u32[]{:S(2)}, u32[]{:S(2)}) collective-permute-start(f32[96,1536]{1,0:T(8,128)} %get-tuple-element.225), channel_id=1, source_target_pairs={{0,2},{2,4},{4,6},{6,0},{1,3},{3,5},{5,7},{7,1},{8,10},{10,12},{12... | collective-permute-start | bytes 1769480 | tf_op jit(solution)/shard_map/ppermute | solution.py:518
  538.7 44.0 %collective-permute-start.31 = (f32[96,1536]{1,0:T(8,128)}, f32[96,1536]{1,0:T(8,128)}, u32[]{:S(2)}, u32[]{:S(2)}) collective-permute-start(f32[96,1536]{1,0:T(8,128)} %get-tuple-element.227), channel_id=1, source_target_pairs={{0,4},{2,6},{4,0},{6,2},{1,5},{3,7},{5,1},{7,3},{8,12},{10,14},{12... | collective-permute-start | bytes 1769480 | tf_op jit(solution)/shard_map/ppermute | solution.py:518
  538.7 44.0 %collective-permute-start.32 = (f32[96,1536]{1,0:T(8,128)}, f32[96,1536]{1,0:T(8,128)}, u32[]{:S(2)}, u32[]{:S(2)}) collective-permute-start(f32[96,1536]{1,0:T(8,128)} %get-tuple-element.226), channel_id=1, source_target_pairs={{0,6},{2,0},{4,2},{6,4},{1,7},{3,1},{5,3},{7,5},{8,14},{10,8},{12,... | collective-permute-start | bytes 1769480 | tf_op jit(solution)/shard_map/ppermute | solution.py:518
  565.7 53.1 %collective-permute-start.29 = (f32[384,1536]{1,0:T(8,128)}, f32[384,1536]{1,0:T(8,128)S(1)}, u32[]{:S(2)}, u32[]{:S(2)}) collective-permute-start(f32[384,1536]{1,0:T(8,128)} %fusion.123), channel_id=1, source_target_pairs={{0,16},{8,24},{16,0},{24,8},{1,17},{9,25},{17,1},{25,9},{2,18},{10... | collective-permute-start | bytes 7077896 | tf_op jit(solution)/shard_map/ppermute | solution.py:471
  638.5 33.3 %collective-permute-start.57 = (f32[384,384]{0,1:T(8,128)S(1)}, f32[384,384]{0,1:T(8,128)S(1)}, u32[]{:S(2)}, u32[]{:S(2)}) collective-permute-start(f32[384,384]{0,1:T(8,128)S(1)} %get-tuple-element.219), channel_id=1, source_target_pairs={{0,8},{8,0},{16,24},{24,16},{1,9},{9,1},{17,25},{25,17},{2,10},{10... | collective-permute-start | bytes 1769480 | tf_op jit(solution)/shard_map/ppermute | solution.py:471
  665.7 37.3 %collective-permute-start.37 = (f32[96,1536]{1,0:T(8,128)S(1)}, f32[96,1536]{1,0:T(8,128)S(1)}, u32[]{:S(2)}, u32[]{:S(2)}) collective-permute-start(f32[96,1536]{1,0:T(8,128)S(1)} %get-tuple-element.221), channel_id=1, source_target_pairs={{0,6},{2,0},{4,2},{6,4},{1,7},{3,1},{5,3},{7,5},{8,14},{10,8},{12,... | collective-permute-start | bytes 1769480 | tf_op jit(solution)/shard_map/ppermute | solution.py:518
  671.8 171.8 %collective-permute-start.33 = (f32[768,768]{1,0:T(8,128)}, f32[768,768]{1,0:T(8,128)}, u32[]{:S(2)}, u32[]{:S(2)}) collective-permute-start(f32[768,768]{1,0:T(8,128)} %add_add_fusion.1), channel_id=1, source_target_pairs={{0,1},{1,0},{2,3},{3,2},{4,5},{5,4},{6,7},{7,6},{8,9},{9,8},{10,11... | collective-permute-start | bytes 7077896 | tf_op jit(solution)/shard_map/ppermute | solution.py:453
  705.4 54.9 %collective-permute-start.38 = (f32[384,512]{1,0:T(8,128)}, f32[384,512]{1,0:T(8,128)}, u32[]{:S(2)}, u32[]{:S(2)}) collective-permute-start(f32[384,512]{1,0:T(8,128)} %fusion.95), channel_id=1, source_target_pairs={{0,8},{8,0},{16,24},{24,16},{1,9},{9,1},{17,25},{25,17},{2,10},{10... | collective-permute-start | bytes 2359304 | tf_op jit(solution)/shard_map/ppermute | solution.py:471
  768.9 32.6 %collective-permute-start.52 = (f32[384,512]{1,0:T(8,128)}, f32[384,512]{1,0:T(8,128)S(1)}, u32[]{:S(2)}, u32[]{:S(2)}) collective-permute-start(f32[384,512]{1,0:T(8,128)} %convolution_add_fusion), channel_id=1, source_target_pairs={{0,16},{8,24},{16,0},{24,8},{1,17},{9,25},{17,1},{25,9},{2,18},{10... | collective-permute-start | bytes 2359304 | tf_op jit(solution)/shard_map/ppermute | solution.py:471
  (164 other events, 2123.3 us)
Sparse Core Ops, SparseCore 0:
  10.9 63.9 all-gather.7
  77.2 51.9 all-gather.9
  131.5 70.4 all-gather.5
where the time goes:
time: 869 us; the launch traced here: 857 us
  waiting for transfers between devices  330 us (38%)
  Pallas kernels  156 us (18%)
  starting transfers between devices  110 us (13%)
  matrix products  109 us (13%)
  other arithmetic  93.7 us (11%)
  local copies, waits for them, and re-layouts  41.5 us (5%)
  between operations  16.1 us (2%)
    ppermute x18, waiting for transfers between devices, chain(): received.append(lax.ppermute(part, 'ctx', [pair]))  173 us
    dot_general x37, matrix products, dot(): lax.dot_general(left, right, ((contract[:1], contract[1:]), ((), ())), pr...  104 us
    ppermute x18, waiting for transfers between devices, over_dp(): lax.ppermute(value, 'dp', [(k, k ^ flip) for k in range(lax.axis_size('dp...  74.6 us
    ppermute x18, starting transfers between devices, scatter_end(): lax.ppermute(give, 'ctx', [(m, (m + k) % n_ctx) for m in range(n_ctx)])  66.8 us
    ppermute x18, waiting for transfers between devices, scatter_end(): lax.ppermute(give, 'ctx', [(m, (m + k) % n_ctx) for m in range(n_ctx)])  64.5 us
    pallas_call x1, Pallas kernels, gather_small(): pl.pallas_call(functools.partial(gather_kernel, sizes), out_shape=jax.Sha...  51 us
    pallas_call x6, Pallas kernels, scan_state(): scan_call(state_kernel, (inner // width,), [pl.BlockSpec((1, tokens, widt...  29 us
    pallas_call x1, Pallas kernels, scan_within_back(): scan_call(within_back_kernel, (seqs, inner // width), [tile, tile, state,...  24.9 us
  transfers between devices with their start and end apart: 67, of which 24 were waited for; matrix products, arithmetic and copies ran while one was open for 20% of the time, Pallas kernels for 17%

commit v1 on v0

--- a/solution.py
+++ b/solution.py
@@ -527,14 +527,17 @@
     count = lax.axis_size("ctx")
     if count == 1:
         return [jnp.zeros_like(part) for part in own]
-    received = entering = list(own)
+    entering = [None] * len(own)
+    leaving = list(own)
     for hop in range(count - 1):
         pair = (count - 1 - hop, count - 2 - hop) if backward else (hop, hop + 1)
-        leaving = own if hop == 0 else [t * r + o for t, r, o in zip(totals, received, own)]
         received = []
-        for part in leaving:
+        for k, part in enumerate(leaving):
+            if k:
+                part, received[k - 1] = tie(part, received[k - 1])
             received.append(lax.ppermute(part, "ctx", [pair]))
         entering = received if hop == 0 else [e + r for e, r in zip(entering, received)]
+        leaving = [t * r + o for t, r, o in zip(totals, received, own)]
     return entering
 
 
@@ -658,7 +661,8 @@
     wx = lax.all_gather(in_proj[:, 1].astype(BF), ("dp", "ctx"), axis=0, tiled=True)
     wz = lax.all_gather(in_proj[:, 0].astype(BF), ("dp", "ctx"), axis=0, tiled=True)
     wo = lax.all_gather(out_proj.astype(BF), ("dp", "ctx"), axis=0, tiled=True)
-    up_own = cotangent.astype(BF)
+    small, late_cotangent = tie(small, cotangent)
+    up_own = late_cotangent.astype(BF)
     if n_t == 2:
         up_away = swap(up_own)
         first = rank == 0
@@ -845,9 +849,7 @@
         grad_norm_gain = lax.dynamic_update_slice_in_dim(
             grad_norm_gain, jnp.sum(product * inverse, axis=(0, 1)), start, 0
         )
-    in_mean = sum_tensor(in_sums)[:, :, None] / width
     scaled_in = normed_grad * own_gain
-    input_grad = cotangent + inverse * scaled_in - own_input * inverse**3 * in_mean
 
     normed_float = normed.astype(F32)
     grad_state_part = dot(normed_float, state_rows, (0, 0), True)
@@ -890,7 +892,11 @@
         ],
         axis=1,
     )
-    far_x = [scatter_high(part, width, near) for part, near in zip(parts_x, near_x)]
+    far_x = []
+    for k, part in enumerate(parts_x):
+        if k:
+            near_x[k], far_x[k - 1] = tie(near_x[k], far_x[k - 1])
+        far_x.append(scatter_high(part, width, near_x[k]))
     grad_x = jnp.concatenate(
         [
             scatter_end(part, width, near, far)
@@ -898,6 +904,10 @@
         ],
         axis=1,
     )
+
+    grad_x, in_sums = tie(grad_x, in_sums)
+    in_mean = sum_tensor(in_sums)[:, :, None] / width
+    input_grad = cotangent + inverse * scaled_in - own_input * inverse**3 * in_mean
 
     def part_tail(start, rows):
         return lax.dynamic_slice_in_dim(tail_part, start, rows, 0)

time: 869 us -> 866 us (level)
  starting transfers between devices: 110 us -> 145 us
  Pallas kernels: 156 us -> 133 us
  waiting for transfers between devices: 330 us -> 310 us
    ppermute x8, waiting for transfers between devices: 8.22 us -> 40.1 us  [swap(): return lax.ppermute(value, 'tensor', [(0, 1), (1, 0)])]
    ppermute x18, waiting for transfers between devices: 173 us -> 142 us  [chain(): received.append(lax.ppermute(part, 'ctx', [pair]))]
    ppermute x18, waiting for transfers between devices: 74.6 us -> 51 us  [over_dp(): lax.ppermute(value, 'dp', [(k, k ^ flip) for k in range(lax.axis_size('dp...]
    pallas_call x1, Pallas kernels: 51 us -> 27.9 us  [gather_small(): pl.pallas_call(functools.partial(gather_kernel, sizes), out_shape=jax.Sha...]
    ppermute x18, starting transfers between devices: 66.8 us -> 89.1 us  [scatter_end(): lax.ppermute(give, 'ctx', [(m, (m + k) % n_ctx) for m in range(n_ctx)])]
    ppermute x18, waiting for transfers between devices: 64.5 us -> 52.2 us  [scatter_end(): lax.ppermute(give, 'ctx', [(m, (m + k) % n_ctx) for m in range(n_ctx)])]
    all_gather x1, waiting for transfers between devices: 0.02 us -> 9.57 us  [on_device(): lax.all_gather(in_proj[:, 1].astype(BF), ('dp', 'ctx'), axis=0, tiled=True)]
    ppermute x18, starting transfers between devices: 21.5 us -> 31 us  [chain(): received.append(lax.ppermute(part, 'ctx', [pair]))]
  transfers between devices with their start and end apart: 67 -> 67, of which waited for: 24 -> 21; matrix products, arithmetic and copies ran while one was open for 20% -> 22% of each run, Pallas kernels for 17% -> 14%
where the time goes in v1:
time: 866 us; the launch traced here: 854 us
  waiting for transfers between devices  310 us (36%)
  starting transfers between devices  145 us (17%)
  Pallas kernels  133 us (15%)
  matrix products  112 us (13%)
  other arithmetic  101 us (12%)
  local copies, waits for them, and re-layouts  35.8 us (4%)
  between operations  16 us (2%)
    ppermute x18, waiting for transfers between devices, chain(): received.append(lax.ppermute(part, 'ctx', [pair]))  142 us
    dot_general x37, matrix products, dot(): lax.dot_general(left, right, ((contract[:1], contract[1:]), ((), ())), pr...  108 us
    ppermute x18, starting transfers between devices, scatter_end(): lax.ppermute(give, 'ctx', [(m, (m + k) % n_ctx) for m in range(n_ctx)])  89.1 us
    ppermute x18, waiting for transfers between devices, scatter_end(): lax.ppermute(give, 'ctx', [(m, (m + k) % n_ctx) for m in range(n_ctx)])  52.2 us
    ppermute x18, waiting for transfers between devices, over_dp(): lax.ppermute(value, 'dp', [(k, k ^ flip) for k in range(lax.axis_size('dp...  51 us
    ppermute x8, waiting for transfers between devices, swap(): return lax.ppermute(value, 'tensor', [(0, 1), (1, 0)])  40.1 us
    ppermute x18, starting transfers between devices, chain(): received.append(lax.ppermute(part, 'ctx', [pair]))  31 us
    pallas_call x6, Pallas kernels, scan_state(): scan_call(state_kernel, (inner // width,), [pl.BlockSpec((1, tokens, widt...  29 us
  transfers between devices with their start and end apart: 67, of which 21 were waited for; matrix products, arithmetic and copies ran while one was open for 22% of the time, Pallas kernels for 14%

profile of v1, /device:TPU:0, one launch (start us, length us, event | category | flops | bytes accessed | tf_op | source)
XLA Modules:
  0.0 853.5 jit_solution(4123649192758438508)
XLA Ops:
  11.3 27.9 %gather_small.1 = bf16[4,4,2,144,128]{4,3,2,1,0:T(8,128)(2,1)} custom-call(bf16[144,128]{1,0:T(8,128)(2,1)} %fusion.148.in_ref), custom_call_target="tpu_custom_call" | custom-call | tf_op jit(solution)/shard_map/gather_small/pallas_call | solution.py:111
  58.9 9.6 %all-gather.8.cloned.1.call-done = bf16[1536,1,1536]{2,0,1:T(8,128)(2,1)} async-done(((bf16[96,1,1536]{2,0,1:T(8,128)(2,1)}), bf16[1536,1,1536]{2,0,1:T(8,128)(2,1)}) %all-gather.8.cloned.1.call-update) | async-done | bytes 4718608 | tf_op jit(solution)/shard_map/all_gather | solution.py:661
  118.1 16.2 %collective-permute-done.1 = f32[1536,128]{1,0:T(8,128)} collective-permute-done((f32[1536,128]{1,0:T(8,128)}, f32[1536,128]{1,0:T(8,128)}, u32[]{:S(2)}, u32[]{:S(2)}) %collective-permute-start.1) | collective-permute-done | bytes 786464 | tf_op jit(solution)/shard_map/ppermute | solution.py:538
  151.8 18.5 %collective-permute-done.2 = f32[1536,128]{1,0:T(8,128)} collective-permute-done((f32[1536,128]{1,0:T(8,128)}, f32[1536,128]{1,0:T(8,128)}, u32[]{:S(2)}, u32[]{:S(2)}) %collective-permute-start.2) | collective-permute-done | bytes 786464 | tf_op jit(solution)/shard_map/ppermute | solution.py:538
  179.4 20.9 %collective-permute-done.4 = f32[1536,128]{1,0:T(8,128)S(1)} collective-permute-done((f32[1536,128]{1,0:T(8,128)S(1)}, f32[1536,128]{1,0:T(8,128)S(1)}, u32[]{:S(2)}, u32[]{:S(2)}) %collective-permute-start.4) | collective-permute-done | bytes 786464 | tf_op jit(solution)/shard_map/ppermute | solution.py:538
  206.9 15.5 %shard_map.336.within_ref = f32[3,256,1536]{2,1,0:T(8,128)} custom-call(bf16[3,256,1536]{2,1,0:T(8,128)(2,1)} %get-tuple-element.281.x_ref.v_ref, bf16[3,256,128]{2,1,0:T(8,128)(2,1)} %get-tuple-element.319.w_ref.u_ref, bf16[3,256,128]{2,1,0:T(8,128)(2,1)} %get-tuple-element.318.r_ref.u_ref, f32[3,256,24]{2,1,0:T(8,128)} %bitcast.244, ...), custom_call_target="tpu_custom_call" | custom-call | flops 4831838208 | bytes 7077888 | tf_op jit(solution)/shard_map/pallas_call | solution.py:395
  231.2 13.7 %shard_map.340 = (f32[3,256,1536]{2,1,0:T(8,128)}, f32[3,256,1536]{2,1,0:T(8,128)}, f32[3,256,1]{2,1,0:T(8,128)}) custom-call(f32[3,256,1536]{2,1,0:T(8,128)} %shard_map.336.within_ref, bf16[3,256,1536]{2,1,0:T(8,128)(2,1)} %get-tuple-element.281.x_ref.v_ref, bf16[3,256,1536]{2,1,0:T(8,128)(2,1)} %bitcast.223, ...), custom_call_target="tpu_custom_call" | custom-call | flops 1207959552 | bytes 18874368 | tf_op jit(solution)/shard_map/pallas_call | solution.py:407
  250.6 10.7 %multiply_reduce_fusion = (f32[1536]{0:T(1024)S(1)}, f32[3,256]{1,0:T(4,128)S(1)}, f32[3,256,1536]{2,1,0:T(8,128)}) fusion(f32[3,256,1536]{2,1,0:T(8,128)} %get-tuple-element.101, f32[3,256]{1,0:T(4,128)S(1)} %get-tuple-element.278, f32[1536]{0:T(1024)S(1)} %dynamic_slice.205, bf16[1536,1536]{1,0:T(8,128)(2,1)} %all-gather.6.cloned.1.call-done, ...), kind=kOutput, calls=%fused_computation.34 | convolution fusion | flops 3635672832 | bytes 16533504 | tf_op jit(solution)/shard_map/dot_general | solution.py:583
  264.9 10.1 %fusion.18 = (bf16[3,256,1536]{2,1,0:T(8,128)(2,1)}, f32[3,256,1536]{2,1,0:T(8,128)}, bf16[3,256,1536]{2,1,0:T(8,128)(2,1)}) fusion(bf16[3,256,1536]{2,1,0:T(8,128)(2,1)} %bitcast.224, f32[3,256,1536]{2,1,0:T(8,128)} %get-tuple-element.104.plain_ref, bf16[3,256,1536]{2,1,0:T(8,128)(2,1)S(1)} %copy-done.1, f32[1536]{0:T(1024)S(1)} %mul.771, ...), kind=kLoop, calls=%fused_computation.25 | loop fusion | flops 28311552 | bytes 28333056 | tf_op jit(solution)/shard_map/convert_element_type | solution.py:761
  302.8 24.9 %shard_map.341 = (f32[3,256,1536]{2,1,0:T(8,128)}, f32[3,256,128]{2,1,0:T(8,128)}, f32[3,256,128]{2,1,0:T(8,128)}) custom-call(f32[3,256,1536]{2,1,0:T(8,128)} %get-tuple-element.284.dy_ref.v_ref, bf16[3,256,1536]{2,1,0:T(8,128)(2,1)} %get-tuple-element.281.x_ref.v_ref, bf16[3,256,128]{2,1,0:T(8,128)(2,1)} %get-tuple-element.319.w_ref.u_ref, ...), custom_call_target="tpu_custom_call" | custom-call | flops 9663676416 | bytes 11796480 | tf_op jit(solution)/shard_map/pallas_call | solution.py:422
  356.2 52.5 %collective-permute-done.20 = f32[1536,128]{1,0:T(8,128)S(1)} collective-permute-done((f32[1536,128]{1,0:T(8,128)S(1)}, f32[1536,128]{1,0:T(8,128)S(1)}, u32[]{:S(2)}, u32[]{:S(2)}) %collective-permute-start.20) | collective-permute-done | bytes 786464 | tf_op jit(solution)/shard_map/ppermute | solution.py:538
  414.8 14.9 %collective-permute-done.22 = f32[1536,128]{1,0:T(8,128)S(1)} collective-permute-done((f32[1536,128]{1,0:T(8,128)S(1)}, f32[1536,128]{1,0:T(8,128)S(1)}, u32[]{:S(2)}, u32[]{:S(2)}) %collective-permute-start.22) | collective-permute-done | bytes 786464 | tf_op jit(solution)/shard_map/ppermute | solution.py:538
  431.2 18.6 %collective-permute-done.23 = f32[1536,128]{1,0:T(8,128)S(1)} collective-permute-done((f32[1536,128]{1,0:T(8,128)S(1)}, f32[1536,128]{1,0:T(8,128)S(1)}, u32[]{:S(2)}, u32[]{:S(2)}) %collective-permute-start.23) | collective-permute-done | bytes 786464 | tf_op jit(solution)/shard_map/ppermute | solution.py:538
  450.1 15.6 %collective-permute-done.24 = f32[384,1536]{1,0:T(8,128)} collective-permute-done((f32[384,1536]{1,0:T(8,128)S(1)}, f32[384,1536]{1,0:T(8,128)}, u32[]{:S(2)}, u32[]{:S(2)}) %collective-permute-start.24) | collective-permute-done | bytes 2359328 | tf_op jit(solution)/shard_map/ppermute | solution.py:471
  466.6 22.0 %shard_map.345 = (f32[3,256,1536]{2,1,0:T(8,128)}, f32[3,256,128]{2,1,0:T(8,128)}, f32[3,256,128]{2,1,0:T(8,128)}, f32[3,256,24]{2,1,0:T(8,128)}, f32[3,256,24]{...) custom-call(f32[3,256,1536]{2,1,0:T(8,128)} %get-tuple-element.284.dy_ref.v_ref, ...), custom_call_target="tpu_custom_call" | custom-call | flops 3623878656 | bytes 25952256 | tf_op jit(solution)/shard_map/pallas_call | solution.py:436
  504.5 11.2 %collective-permute-start.30 = (f32[96,1536]{1,0:T(8,128)}, f32[96,1536]{1,0:T(8,128)}, u32[]{:S(2)}, u32[]{:S(2)}) collective-permute-start(f32[96,1536]{1,0:T(8,128)} %get-tuple-element.293), channel_id=1, source_target_pairs={{0,2},{2,4},{4,6},{6,0},{1,3},{3,5},{5,7},{7,1},{8,10},{10,12},{12... | collective-permute-start | bytes 1769480 | tf_op jit(solution)/shard_map/ppermute | solution.py:518
  533.8 13.8 %collective-permute-done.27 = f32[3,3,1792]{2,1,0:T(4,128)S(1)} collective-permute-done((f32[3,3,1792]{2,1,0:T(4,128)S(1)}, f32[3,3,1792]{2,1,0:T(4,128)S(1)}, u32[]{:S(2)}, u32[]{:S(2)}) %collective-permute-start.27) | collective-permute-done | bytes 64544 | tf_op jit(solution)/shard_map/ppermute | solution.py:449
  568.3 32.1 %collective-permute-done.29 = f32[384,1536]{1,0:T(8,128)S(1)} collective-permute-done((f32[384,1536]{1,0:T(8,128)}, f32[384,1536]{1,0:T(8,128)S(1)}, u32[]{:S(2)}, u32[]{:S(2)}) %collective-permute-start.29) | collective-permute-done | bytes 2359328 | tf_op jit(solution)/shard_map/ppermute | solution.py:471
  636.6 13.9 %collective-permute-start.53 = (f32[96,1536]{1,0:T(8,128)S(1)}, f32[96,1536]{1,0:T(8,128)S(1)}, u32[]{:S(2)}, u32[]{:S(2)}) collective-permute-start(f32[96,1536]{1,0:T(8,128)S(1)} %get-tuple-element.288), channel_id=1, source_target_pairs={{0,2},{2,4},{4,6},{6,0},{1,3},{3,5},{5,7},{7,1},{8,10},{10,12},{12... | collective-permute-start | bytes 1769480 | tf_op jit(solution)/shard_map/ppermute | solution.py:518
  664.2 15.6 %collective-permute-done.54 = f32[96,1536]{1,0:T(8,128)S(1)} collective-permute-done((f32[96,1536]{1,0:T(8,128)S(1)}, f32[96,1536]{1,0:T(8,128)S(1)}, u32[]{:S(2)}, u32[]{:S(2)}) %collective-permute-start.54) | collective-permute-done | bytes 589856 | tf_op jit(solution)/shard_map/ppermute | solution.py:518
  680.2 9.3 %collective-permute-done.55 = f32[96,1536]{1,0:T(8,128)S(1)} collective-permute-done((f32[96,1536]{1,0:T(8,128)S(1)}, f32[96,1536]{1,0:T(8,128)S(1)}, u32[]{:S(2)}, u32[]{:S(2)}) %collective-permute-start.55) | collective-permute-done | bytes 589856 | tf_op jit(solution)/shard_map/ppermute | solution.py:518
  695.1 14.5 %collective-permute-start.61 = (f32[96,384]{0,1:T(8,128)S(1)}, f32[96,384]{0,1:T(8,128)S(1)}, u32[]{:S(2)}, u32[]{:S(2)}) collective-permute-start(f32[96,384]{0,1:T(8,128)S(1)} %get-tuple-element.311), channel_id=1, source_target_pairs={{0,6},{2,0},{4,2},{6,4},{1,7},{3,1},{5,3},{7,5},{8,14},{10,8},{12,... | collective-permute-start | bytes 442376 | tf_op jit(solution)/shard_map/ppermute | solution.py:518
  724.8 39.0 %collective-permute-done.63 = f32[669]{0:T(1024)S(1)} collective-permute-done((f32[669]{0:T(1024)S(1)}, f32[669]{0:T(1024)S(1)}, u32[]{:S(2)}, u32[]{:S(2)}) %collective-permute-start.63) | collective-permute-done | bytes 2708 | tf_op jit(solution)/shard_map/ppermute | solution.py:453
  806.9 9.4 %collective-permute-start.49 = (f32[96,512]{1,0:T(8,128)S(1)}, f32[96,512]{1,0:T(8,128)S(1)}, u32[]{:S(2)}, u32[]{:S(2)}) collective-permute-start(f32[96,512]{1,0:T(8,128)S(1)} %get-tuple-element.305), channel_id=1, source_target_pairs={{0,2},{2,4},{4,6},{6,0},{1,3},{3,5},{5,7},{7,1},{8,10},{10,12},{12... | collective-permute-start | bytes 589832 | tf_op jit(solution)/shard_map/ppermute | solution.py:518
  (584 shorter events, 387.3 us)
Async XLA Ops:
  7.2 61.2 %all-gather.8.cloned.1.call-start = ((), (), s32[]{:S(2)}) async-start(), calls=%async_computation.1 | async-start | bytes 5013504 | tf_op jit(solution)/shard_map/all_gather | solution.py:661
  9.8 134.6 %all-gather.10.cloned.1.call-start = ((), (), s32[]{:S(2)}) async-start(), calls=%async_computation.2 | async-start | bytes 5013504 | tf_op jit(solution)/shard_map/all_gather | solution.py:662
  10.5 240.1 %all-gather.6.cloned.1.call-start = ((), (), s32[]{:S(2)}) async-start(), calls=%async_computation | async-start | bytes 5013504 | tf_op jit(solution)/shard_map/all_gather | solution.py:663
  40.3 207.3 %collective-permute-start.11 = (bf16[3,256,768]{2,1,0:T(8,128)(2,1)}, bf16[3,256,768]{2,1,0:T(8,128)(2,1)}, u32[]{:S(2)}, u32[]{:S(2)}) collective-permute-start(bf16[3,256,768]{2,1,0:T(8,128)(2,1)} %convert_element_type.119), channel_id=1, source_target_pairs={{0,1},{1,0},{2,3},{3,2},{4,5},{5,4},{6,7},{7,6},{8,9},{9,8},{10,11... | collective-permute-start | bytes 3538952 | tf_op jit(solution)/shard_map/ppermute | solution.py:453
  302.3 50.0 %collective-permute-start.14 = (f32[384,1536]{1,0:T(8,128)}, f32[384,1536]{1,0:T(8,128)}, u32[]{:S(2)}, u32[]{:S(2)}) collective-permute-start(f32[384,1536]{1,0:T(8,128)} %fusion.76), channel_id=1, source_target_pairs={{0,8},{8,0},{16,24},{24,16},{1,9},{9,1},{17,25},{25,17},{2,10},{10... | collective-permute-start | bytes 7077896 | tf_op jit(solution)/shard_map/ppermute | solution.py:471
  302.3 50.6 %collective-permute-start.13 = (f32[384,1536]{1,0:T(8,128)}, f32[384,1536]{1,0:T(8,128)}, u32[]{:S(2)}, u32[]{:S(2)}) collective-permute-start(f32[384,1536]{1,0:T(8,128)} %fusion.78), channel_id=1, source_target_pairs={{0,8},{8,0},{16,24},{24,16},{1,9},{9,1},{17,25},{25,17},{2,10},{10... | collective-permute-start | bytes 7077896 | tf_op jit(solution)/shard_map/ppermute | solution.py:471
  328.6 121.5 %collective-permute-start.25 = (f32[384,1536]{1,0:T(8,128)}, f32[384,1536]{1,0:T(8,128)}, u32[]{:S(2)}, u32[]{:S(2)}) collective-permute-start(f32[384,1536]{1,0:T(8,128)} %fusion.134), channel_id=1, source_target_pairs={{0,8},{8,0},{16,24},{24,16},{1,9},{9,1},{17,25},{25,17},{2,10},{10... | collective-permute-start | bytes 7077896 | tf_op jit(solution)/shard_map/ppermute | solution.py:471
  352.4 97.8 %collective-permute-start.26 = (f32[384,1536]{1,0:T(8,128)S(1)}, f32[384,1536]{1,0:T(8,128)}, u32[]{:S(2)}, u32[]{:S(2)}) collective-permute-start(f32[384,1536]{1,0:T(8,128)S(1)} %copy-done.57), channel_id=1, source_target_pairs={{0,8},{8,0},{16,24},{24,16},{1,9},{9,1},{17,25},{25,17},{2,10},{10... | collective-permute-start | bytes 7077896 | tf_op jit(solution)/shard_map/ppermute | solution.py:471
  353.0 215.4 %collective-permute-start.28 = (f32[768,768]{1,0:T(8,128)}, f32[768,768]{1,0:T(8,128)}, u32[]{:S(2)}, u32[]{:S(2)}) collective-permute-start(f32[768,768]{1,0:T(8,128)} %fusion.46), channel_id=1, source_target_pairs={{0,1},{1,0},{2,3},{3,2},{4,5},{5,4},{6,7},{7,6},{8,9},{9,8},{10,11... | collective-permute-start | bytes 7077896 | tf_op jit(solution)/shard_map/ppermute | solution.py:453
  353.7 55.1 %collective-permute-start.20 = (f32[1536,128]{1,0:T(8,128)S(1)}, f32[1536,128]{1,0:T(8,128)S(1)}, u32[]{:S(2)}, u32[]{:S(2)}) collective-permute-start(f32[1536,128]{1,0:T(8,128)S(1)} %multiply_add_fusion.2), channel_id=1, source_target_pairs={{2,0},{3,1},{10,8},{11,9},{18,16},{19,17},{26,24},{27,25}} | collective-permute-start | bytes 2359304 | tf_op jit(solution)/shard_map/ppermute | solution.py:538
  355.3 57.6 %collective-permute-start.21 = (f32[1536,128]{1,0:T(8,128)S(1)}, f32[1536,128]{1,0:T(8,128)S(1)}, u32[]{:S(2)}, u32[]{:S(2)}) collective-permute-start(f32[1536,128]{1,0:T(8,128)S(1)} %multiply_add_fusion.4), channel_id=1, source_target_pairs={{4,2},{5,3},{12,10},{13,11},{20,18},{21,19},{28,26},{29,27}} | collective-permute-start | bytes 2359304 | tf_op jit(solution)/shard_map/ppermute | solution.py:538
  412.8 52.9 %collective-permute-start.24 = (f32[384,1536]{1,0:T(8,128)S(1)}, f32[384,1536]{1,0:T(8,128)}, u32[]{:S(2)}, u32[]{:S(2)}) collective-permute-start(f32[384,1536]{1,0:T(8,128)S(1)} %fusion.73), channel_id=1, source_target_pairs={{0,16},{8,24},{16,0},{24,8},{1,17},{9,25},{17,1},{25,9},{2,18},{10... | collective-permute-start | bytes 7077896 | tf_op jit(solution)/shard_map/ppermute | solution.py:471
  504.5 61.3 %collective-permute-start.30 = (f32[96,1536]{1,0:T(8,128)}, f32[96,1536]{1,0:T(8,128)}, u32[]{:S(2)}, u32[]{:S(2)}) collective-permute-start(f32[96,1536]{1,0:T(8,128)} %get-tuple-element.293), channel_id=1, source_target_pairs={{0,2},{2,4},{4,6},{6,0},{1,3},{3,5},{5,7},{7,1},{8,10},{10,12},{12... | collective-permute-start | bytes 1769480 | tf_op jit(solution)/shard_map/ppermute | solution.py:518
  515.7 50.1 %collective-permute-start.31 = (f32[96,1536]{1,0:T(8,128)}, f32[96,1536]{1,0:T(8,128)}, u32[]{:S(2)}, u32[]{:S(2)}) collective-permute-start(f32[96,1536]{1,0:T(8,128)} %get-tuple-element.295), channel_id=1, source_target_pairs={{0,4},{2,6},{4,0},{6,2},{1,5},{3,7},{5,1},{7,3},{8,12},{10,14},{12... | collective-permute-start | bytes 1769480 | tf_op jit(solution)/shard_map/ppermute | solution.py:518
  515.7 50.1 %collective-permute-start.32 = (f32[96,1536]{1,0:T(8,128)}, f32[96,1536]{1,0:T(8,128)}, u32[]{:S(2)}, u32[]{:S(2)}) collective-permute-start(f32[96,1536]{1,0:T(8,128)} %get-tuple-element.294), channel_id=1, source_target_pairs={{0,6},{2,0},{4,2},{6,4},{1,7},{3,1},{5,3},{7,5},{8,14},{10,8},{12,... | collective-permute-start | bytes 1769480 | tf_op jit(solution)/shard_map/ppermute | solution.py:518
  547.6 52.8 %collective-permute-start.29 = (f32[384,1536]{1,0:T(8,128)}, f32[384,1536]{1,0:T(8,128)S(1)}, u32[]{:S(2)}, u32[]{:S(2)}) collective-permute-start(f32[384,1536]{1,0:T(8,128)} %fusion.123), channel_id=1, source_target_pairs={{0,16},{8,24},{16,0},{24,8},{1,17},{9,25},{17,1},{25,9},{2,18},{10... | collective-permute-start | bytes 7077896 | tf_op jit(solution)/shard_map/ppermute | solution.py:471
  654.2 65.3 %collective-permute-start.35 = (f32[384,512]{1,0:T(8,128)}, f32[384,512]{1,0:T(8,128)}, u32[]{:S(2)}, u32[]{:S(2)}) collective-permute-start(f32[384,512]{1,0:T(8,128)} %fusion.90), channel_id=1, source_target_pairs={{0,8},{8,0},{16,24},{24,16},{1,9},{9,1},{17,25},{25,17},{2,10},{10... | collective-permute-start | bytes 2359304 | tf_op jit(solution)/shard_map/ppermute | solution.py:471
  664.1 55.8 %collective-permute-start.36 = (f32[384,512]{1,0:T(8,128)}, f32[384,512]{1,0:T(8,128)}, u32[]{:S(2)}, u32[]{:S(2)}) collective-permute-start(f32[384,512]{1,0:T(8,128)} %fusion.88), channel_id=1, source_target_pairs={{0,8},{8,0},{16,24},{24,16},{1,9},{9,1},{17,25},{25,17},{2,10},{10... | collective-permute-start | bytes 2359304 | tf_op jit(solution)/shard_map/ppermute | solution.py:471
  679.8 41.5 %collective-permute-start.38 = (f32[384,512]{1,0:T(8,128)}, f32[384,512]{1,0:T(8,128)}, u32[]{:S(2)}, u32[]{:S(2)}) collective-permute-start(f32[384,512]{1,0:T(8,128)} %convolution_add_fusion.4), channel_id=1, source_target_pairs={{0,16},{8,24},{16,0},{24,8},{1,17},{9,25},{17,1},{25,9},{2,18},{10... | collective-permute-start | bytes 2359304 | tf_op jit(solution)/shard_map/ppermute | solution.py:471
  709.8 84.2 %collective-permute-start.33 = (f32[768,768]{1,0:T(8,128)}, f32[768,768]{1,0:T(8,128)}, u32[]{:S(2)}, u32[]{:S(2)}) collective-permute-start(f32[768,768]{1,0:T(8,128)} %add_add_fusion.1), channel_id=1, source_target_pairs={{0,1},{1,0},{2,3},{3,2},{4,5},{5,4},{6,7},{7,6},{8,9},{9,8},{10,11... | collective-permute-start | bytes 7077896 | tf_op jit(solution)/shard_map/ppermute | solution.py:453
  718.2 48.1 %collective-permute-start.34 = (f32[384,512]{1,0:T(8,128)}, f32[384,512]{1,0:T(8,128)}, u32[]{:S(2)}, u32[]{:S(2)}) collective-permute-start(f32[384,512]{1,0:T(8,128)} %fusion.95), channel_id=1, source_target_pairs={{0,8},{8,0},{16,24},{24,16},{1,9},{9,1},{17,25},{25,17},{2,10},{10... | collective-permute-start | bytes 2359304 | tf_op jit(solution)/shard_map/ppermute | solution.py:471
  719.5 57.8 %collective-permute-start.42 = (f32[384,512]{1,0:T(8,128)}, f32[384,512]{1,0:T(8,128)}, u32[]{:S(2)}, u32[]{:S(2)}) collective-permute-start(f32[384,512]{1,0:T(8,128)} %fusion.84), channel_id=1, source_target_pairs={{0,8},{8,0},{16,24},{24,16},{1,9},{9,1},{17,25},{25,17},{2,10},{10... | collective-permute-start | bytes 2359304 | tf_op jit(solution)/shard_map/ppermute | solution.py:471
  720.0 43.8 %collective-permute-start.62 = (f32[48,256]{0,1:T(8,128)S(1)}, f32[48,256]{0,1:T(8,128)S(1)}, u32[]{:S(2)}, u32[]{:S(2)}) collective-permute-start(f32[48,256]{0,1:T(8,128)S(1)} %constant_dynamic-slice_fusion.1), channel_id=1, source_target_pairs={{0,1},{1,0},{2,3},{3,2},{4,5},{5,4},{6,7},{7,6},{8,9},{9,8},{10,11... | collective-permute-start | bytes 147464 | tf_op jit(solution)/shard_map/ppermute | solution.py:453
  721.3 42.5 %collective-permute-start.63 = (f32[669]{0:T(1024)S(1)}, f32[669]{0:T(1024)S(1)}, u32[]{:S(2)}, u32[]{:S(2)}) collective-permute-start(f32[669]{0:T(1024)S(1)} %dynamic_slice.258), channel_id=1, source_target_pairs={{0,1},{1,0},{2,3},{3,2},{4,5},{5,4},{6,7},{7,6},{8,9},{9,8},{10,11... | collective-permute-start | bytes 8036 | tf_op jit(solution)/shard_map/ppermute | solution.py:453
  (163 other events, 2345.0 us)
Sparse Core Ops, SparseCore 0:
  10.9 57.5 all-gather.7
  70.8 54.7 all-gather.9
  127.8 65.1 all-gather.5

commit v2 on v1

--- a/solution.py
+++ b/solution.py
@@ -496,27 +496,62 @@
     return over_dp(first, 1), over_dp(second, 1)
 
 
+def scale_of(value):
+    top = jnp.maximum(jnp.max(jnp.abs(value), axis=0, keepdims=True), 1e-37)
+    return jnp.clip(jnp.floor(14.0 - jnp.log2(top)), -112.0, 100.0)
+
+
+def narrowed(value, exponent):
+    return (value * jnp.exp2(exponent)).astype(jnp.float16)
+
+
+def with_exponent(scaled, exponent):
+    note = jnp.broadcast_to(exponent.astype(jnp.float16), (16, scaled.shape[1]))
+    return jnp.concatenate([scaled, note], axis=0)
+
+
+def widened(packed):
+    rows = packed.shape[0] - 16
+    return packed[:rows].astype(F32) * jnp.exp2(-packed[rows : rows + 1].astype(F32))
+
+
 def scatter_high(part, width, near):
     if not staged():
         return ()
     low, high, rows = row_blocks(width)
-    return over_dp(part((2 * (1 - high) + low) * rows, rows) + near[0], 2)
-
-
-def scatter_end(part, width, near, far):
+    value = part((2 * (1 - high) + low) * rows, rows) + near[0]
+    exponent = scale_of(value)
+    return over_dp(with_exponent(narrowed(value, exponent), exponent), 2)
+
+
+def scatter_ctx(part, width, near, far):
     if not staged():
-        return lax.psum_scatter(
-            part(0, width), ("dp", "ctx"), scatter_dimension=0, tiled=True
+        return (
+            lax.psum_scatter(part(0, width), ("dp", "ctx"), scatter_dimension=0, tiled=True),
+            (),
         )
     low, high, rows = row_blocks(width)
     n_ctx, c = lax.axis_size("ctx"), lax.axis_index("ctx")
-    held = part((2 * high + low) * rows, rows) + near[1] + far
+    held = part((2 * high + low) * rows, rows) + near[1] + widened(far)
     block = rows // n_ctx
-    total = lax.dynamic_slice_in_dim(held, c * block, block, 0)
+    exponent = scale_of(held)
+    scaled = narrowed(held, exponent)
+    sent = []
     for k in range(1, n_ctx):
-        give = lax.dynamic_slice_in_dim(held, lax.rem(c + k, n_ctx) * block, block, 0)
-        total = total + lax.ppermute(give, "ctx", [(m, (m + k) % n_ctx) for m in range(n_ctx)])
+        give = lax.dynamic_slice_in_dim(scaled, lax.rem(c + k, n_ctx) * block, block, 0)
+        give = with_exponent(give, exponent)
+        sent.append(lax.ppermute(give, "ctx", [(m, (m + k) % n_ctx) for m in range(n_ctx)]))
+    return lax.dynamic_slice_in_dim(held, c * block, block, 0), sent
+
+
+def scatter_sum(total, sent):
+    for packed in sent:
+        total = total + widened(packed)
     return total
+
+
+def scatter_end(part, width, near, far):
+    return scatter_sum(*scatter_ctx(part, width, near, far))
 
 
 def tie(first, second):
@@ -526,9 +561,10 @@
 def chain(own, totals, backward):
     count = lax.axis_size("ctx")
     if count == 1:
-        return [jnp.zeros_like(part) for part in own]
+        return [jnp.zeros_like(part) for part in own], own[0]
     entering = [None] * len(own)
     leaving = list(own)
+    mark = own[0]
     for hop in range(count - 1):
         pair = (count - 1 - hop, count - 2 - hop) if backward else (hop, hop + 1)
         received = []
@@ -536,9 +572,11 @@
             if k:
                 part, received[k - 1] = tie(part, received[k - 1])
             received.append(lax.ppermute(part, "ctx", [pair]))
+        if hop == 1:
+            mark = received[0]
         entering = received if hop == 0 else [e + r for e, r in zip(entering, received)]
         leaving = [t * r + o for t, r, o in zip(totals, received, own)]
-    return entering
+    return entering, mark
 
 
 def segment_lengths():
@@ -660,7 +698,6 @@
     small = gather_small(block, sizes)
     wx = lax.all_gather(in_proj[:, 1].astype(BF), ("dp", "ctx"), axis=0, tiled=True)
     wz = lax.all_gather(in_proj[:, 0].astype(BF), ("dp", "ctx"), axis=0, tiled=True)
-    wo = lax.all_gather(out_proj.astype(BF), ("dp", "ctx"), axis=0, tiled=True)
     small, late_cotangent = tie(small, cotangent)
     up_own = late_cotangent.astype(BF)
     if n_t == 2:
@@ -733,7 +770,9 @@
     within = scan_within(act_x, wv, rv, cum, cum_t, jnp.swapaxes(delta, 1, 2))
     own_state, normed_late = tie(own_state, normed)
     zproj = dot(normed_late, wz, (1, 0)).astype(BF).reshape(seqs, tokens, local_inner)
-    entering = chain(own_state, spread, False)
+    entering, mark = chain(own_state, spread, False)
+    out_half = tie(out_proj.astype(BF), mark)[0]
+    wo = lax.all_gather(out_half, ("dp", "ctx"), axis=0, tiled=True)
     entering = jnp.stack(entering, axis=0)
 
     plain, mixed, square_sums = scan_gate(within, act_x, zproj, rv, growth, entering, skip_lanes)
@@ -767,13 +806,13 @@
     dx_bare, near_out = tie(dx_bare, near_out)
     far_out = scatter_high(part_out, width, near_out)
     near_z = scatter_start(part_z, width)
-    leaving = jnp.stack(chain(pulled, spread, True), axis=0)
-    leaving, (far_out, near_z) = tie(leaving, (far_out, near_z))
+    leaving = jnp.stack(chain(pulled, spread, True)[0], axis=0)
+    dx, dw, dr, bare_dot, fade_dot, plain_dot, skip_dot = scan_state_back(
+        dy, act_x, plain, dx_bare, wv, delta, fading, growth, entering, leaving, skip_lanes, dw, dr
+    )
+    dx, (far_out, near_z) = tie(dx, (far_out, near_z))
     far_z = scatter_high(part_z, width, near_z)
     grad_out = scatter_end(part_out, width, near_out, far_out)
-    dx, dw, dr, bare_dot, fade_dot, plain_dot, skip_dot = scan_state_back(
-        dy, act_x, plain, dx_bare, wv, delta, fading, growth, entering, leaving, skip_lanes, dw, dr
-    )
     cum_grad = plain_dot - delta * bare_dot - fading * fade_dot
     end_grad = jnp.sum(fading * fade_dot, axis=1) + totals * jnp.sum(
         (leaving * entering).reshape(seqs, local_heads, HEAD_DIM, STATE), axis=(2, 3)
@@ -808,17 +847,18 @@
             return lax.dynamic_slice_in_dim(weight, start, own_width, 0)
 
         product = dot(x_grad, cut(wx), (1, 1))
+        product_z = dot(z_grad, cut(wz), (1, 1))
         return (
             product
-            + dot(z_grad, cut(wz), (1, 1))
+            + product_z
             + dot(state_rows, cut(ws).astype(F32), (1, 1), True)
             + dot(raw_rows, cut(wd).astype(F32), (1, 1), True)
         )
 
     x_grad, (branch_away, far_z, grad_out) = tie(x_grad, (branch_away, far_z, grad_out))
     layer_output = own_input + (branch + branch_away).reshape(seqs, tokens, own_width)
-    grad_z = scatter_end(part_z, width, near_z, far_z)
-    pieces_x = 3 if local_inner % (3 * LANES) == 0 else 1
+    held_z, sent_z = scatter_ctx(part_z, width, near_z, far_z)
+    pieces_x = 2 if local_inner % (2 * LANES) == 0 else 1
     piece = local_inner // pieces_x
     parts_x = [
         cut_dot(normed, x_grad[:, k * piece : (k + 1) * piece]) for k in range(pieces_x)
@@ -897,15 +937,13 @@
         if k:
             near_x[k], far_x[k - 1] = tie(near_x[k], far_x[k - 1])
         far_x.append(scatter_high(part, width, near_x[k]))
-    grad_x = jnp.concatenate(
-        [
-            scatter_end(part, width, near, far)
-            for part, near, far in zip(parts_x, near_x, far_x)
-        ],
-        axis=1,
-    )
-
-    grad_x, in_sums = tie(grad_x, in_sums)
+    blocks_x = []
+    for k, part in enumerate(parts_x):
+        blocks_x.append(scatter_ctx(part, width, near_x[k], far_x[k]))
+    grad_x = jnp.concatenate([scatter_sum(*block) for block in blocks_x], axis=1)
+
+    grad_x, (in_sums, sent_z) = tie(grad_x, (in_sums, sent_z))
+    grad_z = scatter_sum(held_z, sent_z)
     in_mean = sum_tensor(in_sums)[:, :, None] / width
     input_grad = cotangent + inverse * scaled_in - own_input * inverse**3 * in_mean
 

time: 866 us -> 720 us (0.83)
  waiting for transfers between devices: 310 us -> 213 us
  starting transfers between devices: 145 us -> 84.8 us
  other arithmetic: 101 us -> 112 us
    ppermute x18 -> x15, starting transfers between devices: 89.1 us -> 35.4 us  [scatter_ctx(): lax.ppermute(give, 'ctx', [(m, (m + k) % n_ctx) for m in range(n_ctx)])]
    ppermute x8, waiting for transfers between devices: 40.1 us -> 3.21 us  [swap(): return lax.ppermute(value, 'tensor', [(0, 1), (1, 0)])]
    ppermute x18 -> x15, waiting for transfers between devices: 52.2 us -> 20.4 us  [scatter_ctx(): lax.ppermute(give, 'ctx', [(m, (m + k) % n_ctx) for m in range(n_ctx)])]
    ppermute x18 -> x15, waiting for transfers between devices: 51 us -> 22.9 us  [over_dp(): lax.ppermute(value, 'dp', [(k, k ^ flip) for k in range(lax.axis_size('dp...]
    ppermute x2, waiting for transfers between devices: 15.1 us -> 2.33 us  [from_behind(): lax.ppermute(value, axis, [(source, source + steps) for source in range(i...]
    unnamed x246 -> x274, local copies, waits for them, and re-layouts: 18.5 us -> 23.7 us
    dot_general x37 -> x33, matrix products: 108 us -> 104 us  [dot(): lax.dot_general(left, right, ((contract[:1], contract[1:]), ((), ())), pr...]
  transfers between devices with their start and end apart: 67 -> 61, of which waited for: 21 -> 22; matrix products, arithmetic and copies ran while one was open for 22% -> 30% of each run, Pallas kernels for 14% -> 17%
where the time goes in v2:
time: 720 us; the launch traced here: 709 us
  waiting for transfers between devices  213 us (30%)
  Pallas kernels  133 us (18%)
  other arithmetic  112 us (16%)
  matrix products  106 us (15%)
  starting transfers between devices  84.8 us (12%)
  local copies, waits for them, and re-layouts  43.1 us (6%)
  between operations  16.7 us (2%)
    ppermute x18, waiting for transfers between devices, chain(): received.append(lax.ppermute(part, 'ctx', [pair]))  146 us
    dot_general x33, matrix products, dot(): lax.dot_general(left, right, ((contract[:1], contract[1:]), ((), ())), pr...  104 us
    ppermute x15, starting transfers between devices, scatter_ctx(): lax.ppermute(give, 'ctx', [(m, (m + k) % n_ctx) for m in range(n_ctx)])  35.4 us
    ppermute x18, starting transfers between devices, chain(): received.append(lax.ppermute(part, 'ctx', [pair]))  31.6 us
    pallas_call x6, Pallas kernels, scan_state(): scan_call(state_kernel, (inner // width,), [pl.BlockSpec((1, tokens, widt...  28.9 us
    pallas_call x1, Pallas kernels, gather_small(): pl.pallas_call(functools.partial(gather_kernel, sizes), out_shape=jax.Sha...  28.1 us
    pallas_call x1, Pallas kernels, scan_within_back(): scan_call(within_back_kernel, (seqs, inner // width), [tile, tile, state,...  24.7 us
    unnamed x274, local copies, waits for them, and re-layouts  23.7 us
  transfers between devices with their start and end apart: 61, of which 22 were waited for; matrix products, arithmetic and copies ran while one was open for 30% of the time, Pallas kernels for 17%

profile of v2, /device:TPU:0, one launch (start us, length us, event | category | flops | bytes accessed | tf_op | source)
XLA Modules:
  0.0 708.8 jit_solution(1296452548060785264)
XLA Ops:
  11.1 28.1 %gather_small.1 = bf16[4,4,2,144,128]{4,3,2,1,0:T(8,128)(2,1)} custom-call(bf16[144,128]{1,0:T(8,128)(2,1)} %fusion.143.in_ref), custom_call_target="tpu_custom_call" | custom-call | tf_op jit(solution)/shard_map/gather_small/pallas_call | solution.py:111
  51.4 17.1 %all-gather.8.cloned.1.call-done = bf16[1536,1,1536]{2,0,1:T(8,128)(2,1)} async-done(((bf16[96,1,1536]{2,0,1:T(8,128)(2,1)}), bf16[1536,1,1536]{2,0,1:T(8,128)(2,1)}) %all-gather.8.cloned.1.call-update) | async-done | bytes 4718608 | tf_op jit(solution)/shard_map/all_gather | solution.py:699
  68.6 6.3 fusion.26
  105.5 5.4 collective-permute-start.1
  110.9 23.2 %collective-permute-done.1 = f32[1536,128]{1,0:T(8,128)} collective-permute-done((f32[1536,128]{1,0:T(8,128)}, f32[1536,128]{1,0:T(8,128)}, u32[]{:S(2)}, u32[]{:S(2)}) %collective-permute-start.1) | collective-permute-done | bytes 786464 | tf_op jit(solution)/shard_map/ppermute | solution.py:574
  134.1 5.3 collective-permute-start.2
  145.9 9.3 %collective-permute-done.2 = f32[1536,128]{1,0:T(8,128)} collective-permute-done((f32[1536,128]{1,0:T(8,128)}, f32[1536,128]{1,0:T(8,128)}, u32[]{:S(2)}, u32[]{:S(2)}) %collective-permute-start.2) | collective-permute-done | bytes 786464 | tf_op jit(solution)/shard_map/ppermute | solution.py:574
  177.1 7.5 %fusion.29 = bf16[768,1536]{1,0:T(8,128)(2,1)} fusion(bf16[768,1536]{1,0:T(8,128)(2,1)S(1)} %bitcast.175, bf16[1536,1,1536]{2,0,1:T(8,128)(2,1)} %all-gather.10.cloned.1.call-done), kind=kOutput, calls=%fused_computation.50 | convolution fusion | flops 3625058304 | bytes 9437184 | tf_op jit(solution)/shard_map/dot_general | solution.py:621
  188.4 14.0 %collective-permute-done.4 = f32[1536,128]{1,0:T(8,128)} collective-permute-done((f32[1536,128]{1,0:T(8,128)}, f32[1536,128]{1,0:T(8,128)}, u32[]{:S(2)}, u32[]{:S(2)}) %collective-permute-start.4) | collective-permute-done | bytes 786464 | tf_op jit(solution)/shard_map/ppermute | solution.py:574
  208.1 15.4 %shard_map.336.within_ref = f32[3,256,1536]{2,1,0:T(8,128)} custom-call(bf16[3,256,1536]{2,1,0:T(8,128)(2,1)} %get-tuple-element.284.x_ref.v_ref, bf16[3,256,128]{2,1,0:T(8,128)(2,1)} %get-tuple-element.316.w_ref.u_ref, bf16[3,256,128]{2,1,0:T(8,128)(2,1)} %get-tuple-element.315.r_ref.u_ref, f32[3,256,24]{2,1,0:T(8,128)} %bitcast.248, ...), custom_call_target="tpu_custom_call" | custom-call | flops 4831838208 | bytes 7077888 | tf_op jit(solution)/shard_map/pallas_call | solution.py:395
  231.4 13.7 %shard_map.340 = (f32[3,256,1536]{2,1,0:T(8,128)}, f32[3,256,1536]{2,1,0:T(8,128)}, f32[3,256,1]{2,1,0:T(8,128)}) custom-call(f32[3,256,1536]{2,1,0:T(8,128)} %shard_map.336.within_ref, bf16[3,256,1536]{2,1,0:T(8,128)(2,1)} %get-tuple-element.284.x_ref.v_ref, bf16[3,256,1536]{2,1,0:T(8,128)(2,1)} %bitcast.216, ...), custom_call_target="tpu_custom_call" | custom-call | flops 1207959552 | bytes 18874368 | tf_op jit(solution)/shard_map/pallas_call | solution.py:407
  249.9 10.7 %multiply_reduce_fusion = (f32[1536]{0:T(1024)S(1)}, f32[3,256]{1,0:T(4,128)S(1)}, f32[3,256,1536]{2,1,0:T(8,128)}) fusion(f32[3,256,1536]{2,1,0:T(8,128)} %get-tuple-element.102, f32[3,256]{1,0:T(4,128)S(1)} %get-tuple-element.281, f32[1536]{0:T(1024)S(1)} %dynamic_slice.189, bf16[1536,1536]{1,0:T(8,128)(2,1)} %all-gather.6.cloned.1.call-done, ...), kind=kOutput, calls=%fused_computation.34 | convolution fusion | flops 3635672832 | bytes 16533504 | tf_op jit(solution)/shard_map/dot_general | solution.py:621
  264.2 10.1 %fusion.18 = (bf16[3,256,1536]{2,1,0:T(8,128)(2,1)}, f32[3,256,1536]{2,1,0:T(8,128)}, bf16[3,256,1536]{2,1,0:T(8,128)(2,1)}) fusion(bf16[3,256,1536]{2,1,0:T(8,128)(2,1)} %bitcast.217, f32[3,256,1536]{2,1,0:T(8,128)} %get-tuple-element.106.plain_ref, bf16[3,256,1536]{2,1,0:T(8,128)(2,1)S(1)} %copy-done.1, f32[1536]{0:T(1024)S(1)} %mul.1042, ...), kind=kLoop, calls=%fused_computation.25 | loop fusion | flops 28311552 | bytes 28333056 | tf_op jit(solution)/shard_map/convert_element_type | solution.py:800
  296.7 24.7 %shard_map.341 = (f32[3,256,1536]{2,1,0:T(8,128)}, f32[3,256,128]{2,1,0:T(8,128)}, f32[3,256,128]{2,1,0:T(8,128)}) custom-call(f32[3,256,1536]{2,1,0:T(8,128)} %get-tuple-element.287.dy_ref.v_ref, bf16[3,256,1536]{2,1,0:T(8,128)(2,1)} %get-tuple-element.284.x_ref.v_ref, bf16[3,256,128]{2,1,0:T(8,128)(2,1)} %get-tuple-element.316.w_ref.u_ref, ...), custom_call_target="tpu_custom_call" | custom-call | flops 9663676416 | bytes 11796480 | tf_op jit(solution)/shard_map/pallas_call | solution.py:422
  353.1 67.1 %collective-permute-done.20 = f32[1536,128]{1,0:T(8,128)S(1)} collective-permute-done((f32[1536,128]{1,0:T(8,128)S(1)}, f32[1536,128]{1,0:T(8,128)S(1)}, u32[]{:S(2)}, u32[]{:S(2)}) %collective-permute-start.20) | collective-permute-done | bytes 786464 | tf_op jit(solution)/shard_map/ppermute | solution.py:574
  423.4 16.0 %collective-permute-done.22 = f32[1536,128]{1,0:T(8,128)S(1)} collective-permute-done((f32[1536,128]{1,0:T(8,128)S(1)}, f32[1536,128]{1,0:T(8,128)S(1)}, u32[]{:S(2)}, u32[]{:S(2)}) %collective-permute-start.22) | collective-permute-done | bytes 786464 | tf_op jit(solution)/shard_map/ppermute | solution.py:574
  441.2 16.6 %collective-permute-done.23 = f32[1536,128]{1,0:T(8,128)S(1)} collective-permute-done((f32[1536,128]{1,0:T(8,128)S(1)}, f32[1536,128]{1,0:T(8,128)S(1)}, u32[]{:S(2)}, u32[]{:S(2)}) %collective-permute-start.23) | collective-permute-done | bytes 786464 | tf_op jit(solution)/shard_map/ppermute | solution.py:574
  459.6 21.9 %shard_map.345 = (f32[3,256,1536]{2,1,0:T(8,128)}, f32[3,256,128]{2,1,0:T(8,128)}, f32[3,256,128]{2,1,0:T(8,128)}, f32[3,256,24]{2,1,0:T(8,128)}, f32[3,256,24]{...) custom-call(f32[3,256,1536]{2,1,0:T(8,128)} %get-tuple-element.287.dy_ref.v_ref, ...), custom_call_target="tpu_custom_call" | custom-call | flops 3623878656 | bytes 25952256 | tf_op jit(solution)/shard_map/pallas_call | solution.py:436
  507.9 6.1 multiply_reduce_fusion.4
  532.3 8.4 %fusion.8 = bf16[3,256,1536]{2,1,0:T(8,128)(2,1)S(1)} fusion(f32[3,3,1536]{2,1,0:T(4,128)S(1)} %slice.467, f32[3,256,1536]{2,1,0:T(8,128)} %copy-done.17, f32[1536]{0:T(1024)S(1)} %get-tuple-element.257, f32[1536]{0:T(1024)S(1)} %get-tuple-element.255, f32[1536]{0:T(1024)S(1)} %get-tuple-element.256, f32[1536]{0:T(1024)S(1)} %get-tuple-element.254), kind=kLoop, calls=%fused_computation.15 | loop fusion | flops 12976128 | bytes 7157760 | tf_op jit(solution)/shard_map/convert_element_type | solution.py:841
  589.2 7.4 %collective-permute-done.52 = f16[400,384]{1,0:T(8,128)(2,1)S(1)} collective-permute-done((f16[400,384]{1,0:T(8,128)(2,1)S(1)}, f16[400,384]{1,0:T(8,128)(2,1)S(1)}, u32[]{:S(2)}, u32[]{:S(2)}) %collective-permute-start.52) | collective-permute-done | bytes 307232 | tf_op jit(solution)/shard_map/ppermute | solution.py:471
  635.4 10.9 %collective-permute-done.42 = f16[400,768]{1,0:T(8,128)(2,1)S(1)} collective-permute-done((f16[400,768]{1,0:T(8,128)(2,1)S(1)}, f16[400,768]{1,0:T(8,128)(2,1)S(1)}, u32[]{:S(2)}, u32[]{:S(2)}) %collective-permute-start.42) | collective-permute-done | bytes 614432 | tf_op jit(solution)/shard_map/ppermute | solution.py:471
  654.6 14.5 %collective-permute-start.39 = (f16[112,768]{1,0:T(8,128)(2,1)S(1)}, f16[112,768]{1,0:T(8,128)(2,1)S(1)}, u32[]{:S(2)}, u32[]{:S(2)}) collective-permute-start(f16[112,768]{1,0:T(8,128)(2,1)S(1)} %get-tuple-element.337), channel_id=1, source_target_pairs={{0,2},{2,4},{4,6},{6,0},{1,3},{3,5},{5,7},{7,1},{8,10},{10,12},{12... | collective-permute-start | bytes 516104 | tf_op jit(solution)/shard_map/ppermute | solution.py:543
  679.8 7.4 %collective-permute-done.44 = f16[112,768]{1,0:T(8,128)(2,1)S(1)} collective-permute-done((f16[112,768]{1,0:T(8,128)(2,1)S(1)}, f16[112,768]{1,0:T(8,128)(2,1)S(1)}, u32[]{:S(2)}, u32[]{:S(2)}) %collective-permute-start.44) | collective-permute-done | bytes 172064 | tf_op jit(solution)/shard_map/ppermute | solution.py:543
  (647 shorter events, 325.2 us)
Async XLA Ops:
  7.2 61.4 %all-gather.8.cloned.1.call-start = ((), (), s32[]{:S(2)}) async-start(), calls=%async_computation.1 | async-start | bytes 5013504 | tf_op jit(solution)/shard_map/all_gather | solution.py:699
  9.6 167.5 %all-gather.10.cloned.1.call-start = ((), (), s32[]{:S(2)}) async-start(), calls=%async_computation.2 | async-start | bytes 5013504 | tf_op jit(solution)/shard_map/all_gather | solution.py:700
  10.4 239.5 %all-gather.6.cloned.1.call-start = ((), (), s32[]{:S(2)}) async-start(), calls=%async_computation | async-start | bytes 5013504 | tf_op jit(solution)/shard_map/all_gather | solution.py:775
  105.5 28.6 %collective-permute-start.1 = (f32[1536,128]{1,0:T(8,128)}, f32[1536,128]{1,0:T(8,128)}, u32[]{:S(2)}, u32[]{:S(2)}) collective-permute-start(f32[1536,128]{1,0:T(8,128)} %shard_map.337), channel_id=1, source_target_pairs={{0,2},{1,3},{8,10},{9,11},{16,18},{17,19},{24,26},{25,27}} | collective-permute-start | bytes 2359304 | tf_op jit(solution)/shard_map/ppermute | solution.py:574
  160.5 86.2 %collective-permute-start.11 = (bf16[3,256,768]{2,1,0:T(8,128)(2,1)}, bf16[3,256,768]{2,1,0:T(8,128)(2,1)}, u32[]{:S(2)}, u32[]{:S(2)}) collective-permute-start(bf16[3,256,768]{2,1,0:T(8,128)(2,1)} %convert_element_type.359), channel_id=1, source_target_pairs={{0,1},{1,0},{2,3},{3,2},{4,5},{5,4},{6,7},{7,6},{8,9},{9,8},{10,11... | collective-permute-start | bytes 3538952 | tf_op jit(solution)/shard_map/ppermute | solution.py:453
  171.8 30.5 %collective-permute-start.4 = (f32[1536,128]{1,0:T(8,128)}, f32[1536,128]{1,0:T(8,128)}, u32[]{:S(2)}, u32[]{:S(2)}) collective-permute-start(f32[1536,128]{1,0:T(8,128)} %shard_map.339), channel_id=1, source_target_pairs={{0,2},{1,3},{8,10},{9,11},{16,18},{17,19},{24,26},{25,27}} | collective-permute-start | bytes 2359304 | tf_op jit(solution)/shard_map/ppermute | solution.py:574
  292.6 53.2 %collective-permute-start.14 = (f32[384,1536]{1,0:T(8,128)}, f32[384,1536]{1,0:T(8,128)}, u32[]{:S(2)}, u32[]{:S(2)}) collective-permute-start(f32[384,1536]{1,0:T(8,128)} %fusion.90), channel_id=1, source_target_pairs={{0,8},{8,0},{16,24},{24,16},{1,9},{9,1},{17,25},{25,17},{2,10},{10... | collective-permute-start | bytes 7077896 | tf_op jit(solution)/shard_map/ppermute | solution.py:471
  296.2 50.3 %collective-permute-start.13 = (f32[384,1536]{1,0:T(8,128)}, f32[384,1536]{1,0:T(8,128)}, u32[]{:S(2)}, u32[]{:S(2)}) collective-permute-start(f32[384,1536]{1,0:T(8,128)} %fusion.92), channel_id=1, source_target_pairs={{0,8},{8,0},{16,24},{24,16},{1,9},{9,1},{17,25},{25,17},{2,10},{10... | collective-permute-start | bytes 7077896 | tf_op jit(solution)/shard_map/ppermute | solution.py:471
  326.7 169.0 %collective-permute-start.25 = (f32[384,1536]{1,0:T(8,128)}, f32[384,1536]{1,0:T(8,128)}, u32[]{:S(2)}, u32[]{:S(2)}) collective-permute-start(f32[384,1536]{1,0:T(8,128)} %fusion.113), channel_id=1, source_target_pairs={{0,8},{8,0},{16,24},{24,16},{1,9},{9,1},{17,25},{25,17},{2,10},{10... | collective-permute-start | bytes 7077896 | tf_op jit(solution)/shard_map/ppermute | solution.py:471
  343.2 152.6 %collective-permute-start.26 = (f32[384,1536]{1,0:T(8,128)}, f32[384,1536]{1,0:T(8,128)}, u32[]{:S(2)}, u32[]{:S(2)}) collective-permute-start(f32[384,1536]{1,0:T(8,128)} %fusion.109), channel_id=1, source_target_pairs={{0,8},{8,0},{16,24},{24,16},{1,9},{9,1},{17,25},{25,17},{2,10},{10... | collective-permute-start | bytes 7077896 | tf_op jit(solution)/shard_map/ppermute | solution.py:471
  344.1 206.2 %collective-permute-start.28 = (f32[768,768]{1,0:T(8,128)}, f32[768,768]{1,0:T(8,128)}, u32[]{:S(2)}, u32[]{:S(2)}) collective-permute-start(f32[768,768]{1,0:T(8,128)} %fusion.47), channel_id=1, source_target_pairs={{0,1},{1,0},{2,3},{3,2},{4,5},{5,4},{6,7},{7,6},{8,9},{9,8},{10,11... | collective-permute-start | bytes 7077896 | tf_op jit(solution)/shard_map/ppermute | solution.py:453
  350.5 69.7 %collective-permute-start.20 = (f32[1536,128]{1,0:T(8,128)S(1)}, f32[1536,128]{1,0:T(8,128)S(1)}, u32[]{:S(2)}, u32[]{:S(2)}) collective-permute-start(f32[1536,128]{1,0:T(8,128)S(1)} %multiply_add_fusion.4), channel_id=1, source_target_pairs={{2,0},{3,1},{10,8},{11,9},{18,16},{19,17},{26,24},{27,25}} | collective-permute-start | bytes 2359304 | tf_op jit(solution)/shard_map/ppermute | solution.py:574
  352.1 70.8 %collective-permute-start.21 = (f32[1536,128]{1,0:T(8,128)S(1)}, f32[1536,128]{1,0:T(8,128)S(1)}, u32[]{:S(2)}, u32[]{:S(2)}) collective-permute-start(f32[1536,128]{1,0:T(8,128)S(1)} %multiply_add_fusion.6), channel_id=1, source_target_pairs={{4,2},{5,3},{12,10},{13,11},{20,18},{21,19},{28,26},{29,27}} | collective-permute-start | bytes 2359304 | tf_op jit(solution)/shard_map/ppermute | solution.py:574
  422.9 72.9 %collective-permute-start.24 = (f16[400,1536]{1,0:T(8,128)(2,1)}, f16[400,1536]{1,0:T(8,128)(2,1)}, u32[]{:S(2)}, u32[]{:S(2)}) collective-permute-start(f16[400,1536]{1,0:T(8,128)(2,1)} %pad_maximum_fusion.4), channel_id=1, source_target_pairs={{0,16},{8,24},{16,0},{24,8},{1,17},{9,25},{17,1},{25,9},{2,18},{10... | collective-permute-start | bytes 3686408 | tf_op jit(solution)/shard_map/ppermute | solution.py:471
  502.5 43.1 %collective-permute-start.32 = (f16[112,1536]{1,0:T(8,128)(2,1)}, f16[112,1536]{1,0:T(8,128)(2,1)}, u32[]{:S(2)}, u32[]{:S(2)}) collective-permute-start(f16[112,1536]{1,0:T(8,128)(2,1)} %get-tuple-element.336), channel_id=1, source_target_pairs={{0,6},{2,0},{4,2},{6,4},{1,7},{3,1},{5,3},{7,5},{8,14},{10,8},{12,... | collective-permute-start | bytes 1032200 | tf_op jit(solution)/shard_map/ppermute | solution.py:543
  502.5 43.9 %collective-permute-start.31 = (f16[112,1536]{1,0:T(8,128)(2,1)}, f16[112,1536]{1,0:T(8,128)(2,1)}, u32[]{:S(2)}, u32[]{:S(2)}) collective-permute-start(f16[112,1536]{1,0:T(8,128)(2,1)} %get-tuple-element.335), channel_id=1, source_target_pairs={{0,4},{2,6},{4,0},{6,2},{1,5},{3,7},{5,1},{7,3},{8,12},{10,14},{12... | collective-permute-start | bytes 1032200 | tf_op jit(solution)/shard_map/ppermute | solution.py:543
  503.5 43.7 %collective-permute-start.30 = (f16[112,1536]{1,0:T(8,128)(2,1)S(1)}, f16[112,1536]{1,0:T(8,128)(2,1)}, u32[]{:S(2)}, u32[]{:S(2)}) collective-permute-start(f16[112,1536]{1,0:T(8,128)(2,1)S(1)} %get-tuple-element.334), channel_id=1, source_target_pairs={{0,2},{2,4},{4,6},{6,0},{1,3},{3,5},{5,7},{7,1},{8,10},{10,12},{12... | collective-permute-start | bytes 1032200 | tf_op jit(solution)/shard_map/ppermute | solution.py:543
  560.3 90.9 %collective-permute-start.33 = (f32[768,768]{1,0:T(8,128)}, f32[768,768]{1,0:T(8,128)}, u32[]{:S(2)}, u32[]{:S(2)}) collective-permute-start(f32[768,768]{1,0:T(8,128)} %add_add_fusion), channel_id=1, source_target_pairs={{0,1},{1,0},{2,3},{3,2},{4,5},{5,4},{6,7},{7,6},{8,9},{9,8},{10,11... | collective-permute-start | bytes 7077896 | tf_op jit(solution)/shard_map/ppermute | solution.py:453
  576.0 26.1 %collective-permute-start.37 = (f32[384,768]{1,0:T(8,128)S(1)}, f32[384,768]{1,0:T(8,128)S(1)}, u32[]{:S(2)}, u32[]{:S(2)}) collective-permute-start(f32[384,768]{1,0:T(8,128)S(1)} %copy-done.111), channel_id=1, source_target_pairs={{0,8},{8,0},{16,24},{24,16},{1,9},{9,1},{17,25},{25,17},{2,10},{10... | collective-permute-start | bytes 3538952 | tf_op jit(solution)/shard_map/ppermute | solution.py:471
  576.1 46.5 %collective-permute-start.35 = (f32[384,768]{1,0:T(8,128)}, f32[384,768]{1,0:T(8,128)}, u32[]{:S(2)}, u32[]{:S(2)}) collective-permute-start(f32[384,768]{1,0:T(8,128)} %fusion.72), channel_id=1, source_target_pairs={{0,8},{8,0},{16,24},{24,16},{1,9},{9,1},{17,25},{25,17},{2,10},{10... | collective-permute-start | bytes 3538952 | tf_op jit(solution)/shard_map/ppermute | solution.py:471
  596.6 27.5 %collective-permute-start.36 = (f32[384,768]{1,0:T(8,128)}, f32[384,768]{1,0:T(8,128)}, u32[]{:S(2)}, u32[]{:S(2)}) collective-permute-start(f32[384,768]{1,0:T(8,128)} %fusion.70), channel_id=1, source_target_pairs={{0,8},{8,0},{16,24},{24,16},{1,9},{9,1},{17,25},{25,17},{2,10},{10... | collective-permute-start | bytes 3538952 | tf_op jit(solution)/shard_map/ppermute | solution.py:471
  622.6 65.0 %collective-permute-start.46 = (f16[112,1536]{1,0:T(8,128)(2,1)}, f16[112,1536]{1,0:T(8,128)(2,1)S(1)}, u32[]{:S(2)}, u32[]{:S(2)}) collective-permute-start(f16[112,1536]{1,0:T(8,128)(2,1)} %get-tuple-element.333), channel_id=1, source_target_pairs={{0,2},{2,4},{4,6},{6,0},{1,3},{3,5},{5,7},{7,1},{8,10},{10,12},{12... | collective-permute-start | bytes 1032200 | tf_op jit(solution)/shard_map/ppermute | solution.py:543
  624.2 63.5 %collective-permute-start.47 = (f16[112,1536]{1,0:T(8,128)(2,1)}, f16[112,1536]{1,0:T(8,128)(2,1)S(1)}, u32[]{:S(2)}, u32[]{:S(2)}) collective-permute-start(f16[112,1536]{1,0:T(8,128)(2,1)} %get-tuple-element.332), channel_id=1, source_target_pairs={{0,4},{2,6},{4,0},{6,2},{1,5},{3,7},{5,1},{7,3},{8,12},{10,14},{12... | collective-permute-start | bytes 1032200 | tf_op jit(solution)/shard_map/ppermute | solution.py:543
  627.4 60.2 %collective-permute-start.48 = (f16[112,1536]{1,0:T(8,128)(2,1)}, f16[112,1536]{1,0:T(8,128)(2,1)S(1)}, u32[]{:S(2)}, u32[]{:S(2)}) collective-permute-start(f16[112,1536]{1,0:T(8,128)(2,1)} %get-tuple-element.331), channel_id=1, source_target_pairs={{0,6},{2,0},{4,2},{6,4},{1,7},{3,1},{5,3},{7,5},{8,14},{10,8},{12,... | collective-permute-start | bytes 1032200 | tf_op jit(solution)/shard_map/ppermute | solution.py:543
  (166 other events, 1311.2 us)
Sparse Core Ops, SparseCore 0:
  10.9 57.6 all-gather.7
  70.9 54.6 all-gather.9
  157.8 55.7 all-gather.5

commit v3 on v2

--- a/solution.py
+++ b/solution.py
@@ -387,6 +387,11 @@
     )(v, u, scale)
 
 
+def scan_states(v, u, scale):
+    states = [scan_state(v, u, scale, 0)]
+    return states + [scan_state(v, u, scale, k) for k in range(1, v.shape[0])]
+
+
 def scan_within(x, w, r, cum, cum_t, delta_t):
     seqs, tokens, inner = x.shape
     width = step_width(inner)
@@ -572,7 +577,7 @@
             if k:
                 part, received[k - 1] = tie(part, received[k - 1])
             received.append(lax.ppermute(part, "ctx", [pair]))
-        if hop == 1:
+        if hop == count - 2:
             mark = received[0]
         entering = received if hop == 0 else [e + r for e, r in zip(entering, received)]
         leaving = [t * r + o for t, r, o in zip(totals, received, own)]
@@ -766,9 +771,9 @@
     ]
     cum_t = jnp.swapaxes(cum, 1, 2)
     skip_lanes = jnp.repeat(skip_gain, HEAD_DIM)[None, :]
-    own_state = [scan_state(act_x, wv, fading, k) for k in range(seqs)]
+    own_state = scan_states(act_x, wv, fading)
     within = scan_within(act_x, wv, rv, cum, cum_t, jnp.swapaxes(delta, 1, 2))
-    own_state, normed_late = tie(own_state, normed)
+    own_state[1:], normed_late = tie(own_state[1:], normed)
     zproj = dot(normed_late, wz, (1, 0)).astype(BF).reshape(seqs, tokens, local_inner)
     entering, mark = chain(own_state, spread, False)
     out_half = tie(out_proj.astype(BF), mark)[0]
@@ -800,7 +805,7 @@
     z_grad = (mixed_grad * mixer * silu_grad(gate_input)).astype(BF).reshape(rows, local_inner)
     part_z = cut_dot(normed, z_grad)
 
-    pulled = [scan_state(mixer_grad, rv, growth, k) for k in range(seqs)]
+    pulled = scan_states(mixer_grad, rv, growth)
     dy = mixer_grad
     dx_bare, dw, dr = scan_within_back(dy, act_x, wv, rv, cum, cum_t, delta)
     dx_bare, near_out = tie(dx_bare, near_out)
@@ -810,7 +815,7 @@
     dx, dw, dr, bare_dot, fade_dot, plain_dot, skip_dot = scan_state_back(
         dy, act_x, plain, dx_bare, wv, delta, fading, growth, entering, leaving, skip_lanes, dw, dr
     )
-    dx, (far_out, near_z) = tie(dx, (far_out, near_z))
+    dx, (far_out, near_z, branch) = tie(dx, (far_out, near_z, branch))
     far_z = scatter_high(part_z, width, near_z)
     grad_out = scatter_end(part_out, width, near_out, far_out)
     cum_grad = plain_dot - delta * bare_dot - fading * fade_dot
@@ -872,12 +877,12 @@
         starts = [k * own_width for k in range(n_t)]
     columns = [normed_columns(start) for start in starts]
     if n_t == 2:
-        normed_grad = columns[1] + swap(columns[0])
+        normed_grad, normed_away = columns[1], swap(columns[0])
     else:
         normed_grad = lax.psum_scatter(
             jnp.concatenate(columns, axis=1), "tensor", scatter_dimension=1, tiled=True
         )
-    normed_grad = normed_grad.reshape(seqs, tokens, own_width)
+        normed_away = jnp.zeros((1,), F32)
     own_gain = lax.dynamic_slice_in_dim(norm_gain, rank * own_width, own_width, 0)
     grad_norm_gain = jnp.zeros((D,), F32)
     in_sums = 0.0
@@ -889,7 +894,6 @@
         grad_norm_gain = lax.dynamic_update_slice_in_dim(
             grad_norm_gain, jnp.sum(product * inverse, axis=(0, 1)), start, 0
         )
-    scaled_in = normed_grad * own_gain
 
     normed_float = normed.astype(F32)
     grad_state_part = dot(normed_float, state_rows, (0, 0), True)
@@ -942,7 +946,8 @@
         blocks_x.append(scatter_ctx(part, width, near_x[k], far_x[k]))
     grad_x = jnp.concatenate([scatter_sum(*block) for block in blocks_x], axis=1)
 
-    grad_x, (in_sums, sent_z) = tie(grad_x, (in_sums, sent_z))
+    grad_x, (in_sums, sent_z, normed_away) = tie(grad_x, (in_sums, sent_z, normed_away))
+    scaled_in = (normed_grad + normed_away).reshape(seqs, tokens, own_width) * own_gain
     grad_z = scatter_sum(held_z, sent_z)
     in_mean = sum_tensor(in_sums)[:, :, None] / width
     input_grad = cotangent + inverse * scaled_in - own_input * inverse**3 * in_mean

time: 720 us -> 723 us (level)
    ppermute x15, waiting for transfers between devices: 20.4 us -> 37 us  [scatter_ctx(): lax.ppermute(give, 'ctx', [(m, (m + k) % n_ctx) for m in range(n_ctx)])]
    ppermute x15, waiting for transfers between devices: 22.9 us -> 14.2 us  [over_dp(): lax.ppermute(value, 'dp', [(k, k ^ flip) for k in range(lax.axis_size('dp...]
    ppermute x15, starting transfers between devices: 35.4 us -> 28 us  [scatter_ctx(): lax.ppermute(give, 'ctx', [(m, (m + k) % n_ctx) for m in range(n_ctx)])]
    unnamed x274 -> x304, local copies, waits for them, and re-layouts: 23.7 us -> 20.2 us
  transfers between devices with their start and end apart: 61 -> 61, of which waited for: 22 -> 24; matrix products, arithmetic and copies ran while one was open for 30% -> 31% of each run, Pallas kernels for 17% -> 13%
where the time goes in v3:
time: 723 us; the launch traced here: 712 us
  waiting for transfers between devices  220 us (30%)
  Pallas kernels  133 us (18%)
  other arithmetic  117 us (16%)
  matrix products  99.5 us (14%)
  starting transfers between devices  79.3 us (11%)
  local copies, waits for them, and re-layouts  45.4 us (6%)
  between operations  16.9 us (2%)
    ppermute x18, waiting for transfers between devices, chain(): received.append(lax.ppermute(part, 'ctx', [pair]))  147 us
    dot_general x33, matrix products, dot(): lax.dot_general(left, right, ((contract[:1], contract[1:]), ((), ())), pr...  97.3 us
    ppermute x15, waiting for transfers between devices, scatter_ctx(): lax.ppermute(give, 'ctx', [(m, (m + k) % n_ctx) for m in range(n_ctx)])  37 us
    ppermute x18, starting transfers between devices, chain(): received.append(lax.ppermute(part, 'ctx', [pair]))  31 us
    pallas_call x6, Pallas kernels, scan_state(): scan_call(state_kernel, (inner // width,), [pl.BlockSpec((1, tokens, widt...  28.8 us
    ppermute x15, starting transfers between devices, scatter_ctx(): lax.ppermute(give, 'ctx', [(m, (m + k) % n_ctx) for m in range(n_ctx)])  28 us
    pallas_call x1, Pallas kernels, gather_small(): pl.pallas_call(functools.partial(gather_kernel, sizes), out_shape=jax.Sha...  28 us
    pallas_call x1, Pallas kernels, scan_within_back(): scan_call(within_back_kernel, (seqs, inner // width), [tile, tile, state,...  24.7 us
  transfers between devices with their start and end apart: 61, of which 24 were waited for; matrix products, arithmetic and copies ran while one was open for 31% of the time, Pallas kernels for 13%

profile of v3, /device:TPU:0, one launch (start us, length us, event | category | flops | bytes accessed | tf_op | source)
XLA Modules:
  0.0 711.7 jit_solution(14324698744833586626)
XLA Ops:
  11.1 28.0 %gather_small.1 = bf16[4,4,2,144,128]{4,3,2,1,0:T(8,128)(2,1)} custom-call(bf16[144,128]{1,0:T(8,128)(2,1)} %fusion.143.in_ref), custom_call_target="tpu_custom_call" | custom-call | tf_op jit(solution)/shard_map/gather_small/pallas_call | solution.py:111
  55.6 12.9 %all-gather.8.cloned.1.call-done = bf16[1536,1,1536]{2,0,1:T(8,128)(2,1)} async-done(((bf16[96,1,1536]{2,0,1:T(8,128)(2,1)}), bf16[1536,1,1536]{2,0,1:T(8,128)(2,1)}) %all-gather.8.cloned.1.call-update) | async-done | bytes 4718608 | tf_op jit(solution)/shard_map/all_gather | solution.py:704
  68.5 6.3 fusion.26
  111.7 21.2 %collective-permute-done.1 = f32[1536,128]{1,0:T(8,128)} collective-permute-done((f32[1536,128]{1,0:T(8,128)}, f32[1536,128]{1,0:T(8,128)}, u32[]{:S(2)}, u32[]{:S(2)}) %collective-permute-start.1) | collective-permute-done | bytes 786464 | tf_op jit(solution)/shard_map/ppermute | solution.py:579
  144.6 9.8 %collective-permute-done.2 = f32[1536,128]{1,0:T(8,128)} collective-permute-done((f32[1536,128]{1,0:T(8,128)}, f32[1536,128]{1,0:T(8,128)}, u32[]{:S(2)}, u32[]{:S(2)}) %collective-permute-start.2) | collective-permute-done | bytes 786464 | tf_op jit(solution)/shard_map/ppermute | solution.py:579
  164.7 10.2 %collective-permute-done.4 = f32[1536,128]{1,0:T(8,128)S(1)} collective-permute-done((f32[1536,128]{1,0:T(8,128)}, f32[1536,128]{1,0:T(8,128)S(1)}, u32[]{:S(2)}, u32[]{:S(2)}) %collective-permute-start.4) | collective-permute-done | bytes 786464 | tf_op jit(solution)/shard_map/ppermute | solution.py:579
  193.6 7.4 %fusion.29 = bf16[768,1536]{1,0:T(8,128)(2,1)} fusion(bf16[768,1536]{1,0:T(8,128)(2,1)S(1)} %bitcast.175, bf16[1536,1,1536]{2,0,1:T(8,128)(2,1)} %all-gather.10.cloned.1.call-done), kind=kOutput, calls=%fused_computation.50 | convolution fusion | flops 3625058304 | bytes 9437184 | tf_op jit(solution)/shard_map/dot_general | solution.py:626
  201.7 15.6 %shard_map.336.within_ref = f32[3,256,1536]{2,1,0:T(8,128)} custom-call(bf16[3,256,1536]{2,1,0:T(8,128)(2,1)} %get-tuple-element.286.x_ref.v_ref, bf16[3,256,128]{2,1,0:T(8,128)(2,1)} %get-tuple-element.318.w_ref.u_ref, bf16[3,256,128]{2,1,0:T(8,128)(2,1)} %get-tuple-element.317.r_ref.u_ref, f32[3,256,24]{2,1,0:T(8,128)} %bitcast.248, ...), custom_call_target="tpu_custom_call" | custom-call | flops 4831838208 | bytes 7077888 | tf_op jit(solution)/shard_map/pallas_call | solution.py:400
  226.0 13.9 %shard_map.340 = (f32[3,256,1536]{2,1,0:T(8,128)}, f32[3,256,1536]{2,1,0:T(8,128)}, f32[3,256,1]{2,1,0:T(8,128)}) custom-call(f32[3,256,1536]{2,1,0:T(8,128)} %shard_map.336.within_ref, bf16[3,256,1536]{2,1,0:T(8,128)(2,1)} %get-tuple-element.286.x_ref.v_ref, bf16[3,256,1536]{2,1,0:T(8,128)(2,1)} %bitcast.217, ...), custom_call_target="tpu_custom_call" | custom-call | flops 1207959552 | bytes 18874368 | tf_op jit(solution)/shard_map/pallas_call | solution.py:412
  244.9 10.7 %multiply_reduce_fusion = (f32[1536]{0:T(1024)S(1)}, f32[3,256]{1,0:T(4,128)S(1)}, f32[3,256,1536]{2,1,0:T(8,128)}) fusion(f32[3,256,1536]{2,1,0:T(8,128)} %get-tuple-element.105, f32[3,256]{1,0:T(4,128)S(1)} %get-tuple-element.283, f32[1536]{0:T(1024)S(1)} %dynamic_slice.189, bf16[1536,1536]{1,0:T(8,128)(2,1)} %all-gather.6.cloned.1.call-done, ...), kind=kOutput, calls=%fused_computation.34 | convolution fusion | flops 3635672832 | bytes 16533504 | tf_op jit(solution)/shard_map/dot_general | solution.py:626
  259.2 10.1 %fusion.18 = (bf16[3,256,1536]{2,1,0:T(8,128)(2,1)}, f32[3,256,1536]{2,1,0:T(8,128)}, bf16[3,256,1536]{2,1,0:T(8,128)(2,1)}) fusion(bf16[3,256,1536]{2,1,0:T(8,128)(2,1)} %bitcast.218, f32[3,256,1536]{2,1,0:T(8,128)} %get-tuple-element.106.plain_ref, bf16[3,256,1536]{2,1,0:T(8,128)(2,1)S(1)} %copy-done.1, f32[1536]{0:T(1024)S(1)} %mul.1042, ...), kind=kLoop, calls=%fused_computation.25 | loop fusion | flops 28311552 | bytes 28333056 | tf_op jit(solution)/shard_map/convert_element_type | solution.py:805
  283.9 24.7 %shard_map.341 = (f32[3,256,1536]{2,1,0:T(8,128)}, f32[3,256,128]{2,1,0:T(8,128)}, f32[3,256,128]{2,1,0:T(8,128)}) custom-call(f32[3,256,1536]{2,1,0:T(8,128)} %get-tuple-element.289.dy_ref.v_ref, bf16[3,256,1536]{2,1,0:T(8,128)(2,1)} %get-tuple-element.286.x_ref.v_ref, bf16[3,256,128]{2,1,0:T(8,128)(2,1)} %get-tuple-element.318.w_ref.u_ref, ...), custom_call_target="tpu_custom_call" | custom-call | flops 9663676416 | bytes 11796480 | tf_op jit(solution)/shard_map/pallas_call | solution.py:427
  344.0 72.2 %collective-permute-done.20 = f32[1536,128]{1,0:T(8,128)S(1)} collective-permute-done((f32[1536,128]{1,0:T(8,128)S(1)}, f32[1536,128]{1,0:T(8,128)S(1)}, u32[]{:S(2)}, u32[]{:S(2)}) %collective-permute-start.20) | collective-permute-done | bytes 786464 | tf_op jit(solution)/shard_map/ppermute | solution.py:579
  419.9 16.3 %collective-permute-done.22 = f32[1536,128]{1,0:T(8,128)S(1)} collective-permute-done((f32[1536,128]{1,0:T(8,128)S(1)}, f32[1536,128]{1,0:T(8,128)S(1)}, u32[]{:S(2)}, u32[]{:S(2)}) %collective-permute-start.22) | collective-permute-done | bytes 786464 | tf_op jit(solution)/shard_map/ppermute | solution.py:579
  438.2 17.4 %collective-permute-done.23 = f32[1536,128]{1,0:T(8,128)S(1)} collective-permute-done((f32[1536,128]{1,0:T(8,128)S(1)}, f32[1536,128]{1,0:T(8,128)S(1)}, u32[]{:S(2)}, u32[]{:S(2)}) %collective-permute-start.23) | collective-permute-done | bytes 786464 | tf_op jit(solution)/shard_map/ppermute | solution.py:579
  457.4 21.8 %shard_map.345 = (f32[3,256,1536]{2,1,0:T(8,128)}, f32[3,256,128]{2,1,0:T(8,128)}, f32[3,256,128]{2,1,0:T(8,128)}, f32[3,256,24]{2,1,0:T(8,128)}, f32[3,256,24]{...) custom-call(f32[3,256,1536]{2,1,0:T(8,128)} %get-tuple-element.289.dy_ref.v_ref, ...), custom_call_target="tpu_custom_call" | custom-call | flops 3623878656 | bytes 25952256 | tf_op jit(solution)/shard_map/pallas_call | solution.py:441
  495.1 6.1 multiply_reduce_fusion.4
  531.4 8.3 %fusion.8 = bf16[3,256,1536]{2,1,0:T(8,128)(2,1)S(1)} fusion(f32[3,3,1536]{2,1,0:T(4,128)S(1)} %slice.467, f32[3,256,1536]{2,1,0:T(8,128)} %copy-done.15, f32[1536]{0:T(1024)S(1)} %copy-done.87, f32[1536]{0:T(1024)S(1)} %copy-done.83, f32[1536]{0:T(1024)S(1)} %copy-done.85, f32[1536]{0:T(1024)S(1)} %get-tuple-element.256), kind=kLoop, calls=%fused_computation.15 | loop fusion | flops 12976128 | bytes 7157760 | tf_op jit(solution)/shard_map/convert_element_type | solution.py:846
  598.8 5.9 collective-permute-done.54
  604.8 6.2 collective-permute-done.53
  633.0 11.8 %collective-permute-done.41 = f16[400,768]{1,0:T(8,128)(2,1)S(1)} collective-permute-done((f16[400,768]{1,0:T(8,128)(2,1)S(1)}, f16[400,768]{1,0:T(8,128)(2,1)S(1)}, u32[]{:S(2)}, u32[]{:S(2)}) %collective-permute-start.41) | collective-permute-done | bytes 614432 | tf_op jit(solution)/shard_map/ppermute | solution.py:476
  654.0 9.0 %collective-permute-start.42 = (f16[112,768]{1,0:T(8,128)(2,1)S(1)}, f16[112,768]{1,0:T(8,128)(2,1)S(1)}, u32[]{:S(2)}, u32[]{:S(2)}) collective-permute-start(f16[112,768]{1,0:T(8,128)(2,1)S(1)} %get-tuple-element.342), channel_id=1, source_target_pairs={{0,2},{2,4},{4,6},{6,0},{1,3},{3,5},{5,7},{7,1},{8,10},{10,12},{12... | collective-permute-start | bytes 516104 | tf_op jit(solution)/shard_map/ppermute | solution.py:548
  672.6 7.6 %collective-permute-done.39 = f16[112,768]{1,0:T(8,128)(2,1)S(1)} collective-permute-done((f16[112,768]{1,0:T(8,128)(2,1)S(1)}, f16[112,768]{1,0:T(8,128)(2,1)S(1)}, u32[]{:S(2)}, u32[]{:S(2)}) %collective-permute-start.39) | collective-permute-done | bytes 172064 | tf_op jit(solution)/shard_map/ppermute | solution.py:548
  681.5 6.2 collective-permute-done.47
  (678 shorter events, 335.3 us)
Async XLA Ops:
  7.2 61.3 %all-gather.8.cloned.1.call-start = ((), (), s32[]{:S(2)}) async-start(), calls=%async_computation.1 | async-start | bytes 5013504 | tf_op jit(solution)/shard_map/all_gather | solution.py:704
  9.6 184.0 %all-gather.10.cloned.1.call-start = ((), (), s32[]{:S(2)}) async-start(), calls=%async_computation.2 | async-start | bytes 5013504 | tf_op jit(solution)/shard_map/all_gather | solution.py:705
  10.4 234.5 %all-gather.6.cloned.1.call-start = ((), (), s32[]{:S(2)}) async-start(), calls=%async_computation | async-start | bytes 5013504 | tf_op jit(solution)/shard_map/all_gather | solution.py:780
  96.9 36.0 %collective-permute-start.1 = (f32[1536,128]{1,0:T(8,128)}, f32[1536,128]{1,0:T(8,128)}, u32[]{:S(2)}, u32[]{:S(2)}) collective-permute-start(f32[1536,128]{1,0:T(8,128)} %shard_map.339), channel_id=1, source_target_pairs={{0,2},{1,3},{8,10},{9,11},{16,18},{17,19},{24,26},{25,27}} | collective-permute-start | bytes 2359304 | tf_op jit(solution)/shard_map/ppermute | solution.py:579
  180.1 61.5 %collective-permute-start.11 = (bf16[3,256,768]{2,1,0:T(8,128)(2,1)}, bf16[3,256,768]{2,1,0:T(8,128)(2,1)}, u32[]{:S(2)}, u32[]{:S(2)}) collective-permute-start(bf16[3,256,768]{2,1,0:T(8,128)(2,1)} %convert_element_type.357), channel_id=1, source_target_pairs={{0,1},{1,0},{2,3},{3,2},{4,5},{5,4},{6,7},{7,6},{8,9},{9,8},{10,11... | collective-permute-start | bytes 3538952 | tf_op jit(solution)/shard_map/ppermute | solution.py:458
  192.0 25.2 %collective-permute-start.7 = (f32[1536,128]{1,0:T(8,128)}, f32[1536,128]{1,0:T(8,128)}, u32[]{:S(2)}, u32[]{:S(2)}) collective-permute-start(f32[1536,128]{1,0:T(8,128)} %multiply_add_fusion.12), channel_id=1, source_target_pairs={{2,4},{3,5},{10,12},{11,13},{18,20},{19,21},{26,28},{27,29}} | collective-permute-start | bytes 2359304 | tf_op jit(solution)/shard_map/ppermute | solution.py:579
  310.9 27.5 %collective-permute-start.13 = (f32[384,1536]{1,0:T(8,128)S(1)}, f32[384,1536]{1,0:T(8,128)S(1)}, u32[]{:S(2)}, u32[]{:S(2)}) collective-permute-start(f32[384,1536]{1,0:T(8,128)S(1)} %fusion.92), channel_id=1, source_target_pairs={{0,8},{8,0},{16,24},{24,16},{1,9},{9,1},{17,25},{25,17},{2,10},{10... | collective-permute-start | bytes 7077896 | tf_op jit(solution)/shard_map/ppermute | solution.py:476
  312.2 27.0 %collective-permute-start.14 = (f32[384,1536]{1,0:T(8,128)S(1)}, f32[384,1536]{1,0:T(8,128)S(1)}, u32[]{:S(2)}, u32[]{:S(2)}) collective-permute-start(f32[384,1536]{1,0:T(8,128)S(1)} %fusion.90), channel_id=1, source_target_pairs={{0,8},{8,0},{16,24},{24,16},{1,9},{9,1},{17,25},{25,17},{2,10},{10... | collective-permute-start | bytes 7077896 | tf_op jit(solution)/shard_map/ppermute | solution.py:476
  316.1 178.9 %collective-permute-start.25 = (f32[384,1536]{1,0:T(8,128)}, f32[384,1536]{1,0:T(8,128)}, u32[]{:S(2)}, u32[]{:S(2)}) collective-permute-start(f32[384,1536]{1,0:T(8,128)} %fusion.113), channel_id=1, source_target_pairs={{0,8},{8,0},{16,24},{24,16},{1,9},{9,1},{17,25},{25,17},{2,10},{10... | collective-permute-start | bytes 7077896 | tf_op jit(solution)/shard_map/ppermute | solution.py:476
  336.2 158.8 %collective-permute-start.26 = (f32[384,1536]{1,0:T(8,128)}, f32[384,1536]{1,0:T(8,128)}, u32[]{:S(2)}, u32[]{:S(2)}) collective-permute-start(f32[384,1536]{1,0:T(8,128)} %fusion.109), channel_id=1, source_target_pairs={{0,8},{8,0},{16,24},{24,16},{1,9},{9,1},{17,25},{25,17},{2,10},{10... | collective-permute-start | bytes 7077896 | tf_op jit(solution)/shard_map/ppermute | solution.py:476
  336.8 212.8 %collective-permute-start.28 = (f32[768,768]{1,0:T(8,128)}, f32[768,768]{1,0:T(8,128)}, u32[]{:S(2)}, u32[]{:S(2)}) collective-permute-start(f32[768,768]{1,0:T(8,128)} %fusion.47), channel_id=1, source_target_pairs={{0,1},{1,0},{2,3},{3,2},{4,5},{5,4},{6,7},{7,6},{8,9},{9,8},{10,11... | collective-permute-start | bytes 7077896 | tf_op jit(solution)/shard_map/ppermute | solution.py:458
  341.4 74.7 %collective-permute-start.20 = (f32[1536,128]{1,0:T(8,128)S(1)}, f32[1536,128]{1,0:T(8,128)S(1)}, u32[]{:S(2)}, u32[]{:S(2)}) collective-permute-start(f32[1536,128]{1,0:T(8,128)S(1)} %multiply_add_fusion.4), channel_id=1, source_target_pairs={{2,0},{3,1},{10,8},{11,9},{18,16},{19,17},{26,24},{27,25}} | collective-permute-start | bytes 2359304 | tf_op jit(solution)/shard_map/ppermute | solution.py:579
  343.0 75.8 %collective-permute-start.21 = (f32[1536,128]{1,0:T(8,128)S(1)}, f32[1536,128]{1,0:T(8,128)S(1)}, u32[]{:S(2)}, u32[]{:S(2)}) collective-permute-start(f32[1536,128]{1,0:T(8,128)S(1)} %multiply_add_fusion.6), channel_id=1, source_target_pairs={{4,2},{5,3},{12,10},{13,11},{20,18},{21,19},{28,26},{29,27}} | collective-permute-start | bytes 2359304 | tf_op jit(solution)/shard_map/ppermute | solution.py:579
  418.8 76.2 %collective-permute-start.24 = (f16[400,1536]{1,0:T(8,128)(2,1)}, f16[400,1536]{1,0:T(8,128)(2,1)}, u32[]{:S(2)}, u32[]{:S(2)}) collective-permute-start(f16[400,1536]{1,0:T(8,128)(2,1)} %pad_maximum_fusion.4), channel_id=1, source_target_pairs={{0,16},{8,24},{16,0},{24,8},{1,17},{9,25},{17,1},{25,9},{2,18},{10... | collective-permute-start | bytes 3686408 | tf_op jit(solution)/shard_map/ppermute | solution.py:476
  507.7 41.9 %collective-permute-start.29 = (f16[400,1536]{1,0:T(8,128)(2,1)}, f16[400,1536]{1,0:T(8,128)(2,1)}, u32[]{:S(2)}, u32[]{:S(2)}) collective-permute-start(f16[400,1536]{1,0:T(8,128)(2,1)} %pad_maximum_fusion.5), channel_id=1, source_target_pairs={{0,16},{8,24},{16,0},{24,8},{1,17},{9,25},{17,1},{25,9},{2,18},{10... | collective-permute-start | bytes 3686408 | tf_op jit(solution)/shard_map/ppermute | solution.py:476
  515.0 29.7 %collective-permute-start.32 = (f16[112,1536]{1,0:T(8,128)(2,1)}, f16[112,1536]{1,0:T(8,128)(2,1)}, u32[]{:S(2)}, u32[]{:S(2)}) collective-permute-start(f16[112,1536]{1,0:T(8,128)(2,1)} %get-tuple-element.338), channel_id=1, source_target_pairs={{0,6},{2,0},{4,2},{6,4},{1,7},{3,1},{5,3},{7,5},{8,14},{10,8},{12,... | collective-permute-start | bytes 1032200 | tf_op jit(solution)/shard_map/ppermute | solution.py:548
  515.0 31.4 %collective-permute-start.31 = (f16[112,1536]{1,0:T(8,128)(2,1)}, f16[112,1536]{1,0:T(8,128)(2,1)}, u32[]{:S(2)}, u32[]{:S(2)}) collective-permute-start(f16[112,1536]{1,0:T(8,128)(2,1)} %get-tuple-element.337), channel_id=1, source_target_pairs={{0,4},{2,6},{4,0},{6,2},{1,5},{3,7},{5,1},{7,3},{8,12},{10,14},{12... | collective-permute-start | bytes 1032200 | tf_op jit(solution)/shard_map/ppermute | solution.py:548
  554.7 68.2 %collective-permute-start.34 = (f32[384,768]{1,0:T(8,128)}, f32[384,768]{1,0:T(8,128)}, u32[]{:S(2)}, u32[]{:S(2)}) collective-permute-start(f32[384,768]{1,0:T(8,128)} %fusion.72), channel_id=1, source_target_pairs={{0,8},{8,0},{16,24},{24,16},{1,9},{9,1},{17,25},{25,17},{2,10},{10... | collective-permute-start | bytes 3538952 | tf_op jit(solution)/shard_map/ppermute | solution.py:476
  554.7 68.2 %collective-permute-start.35 = (f32[384,768]{1,0:T(8,128)}, f32[384,768]{1,0:T(8,128)}, u32[]{:S(2)}, u32[]{:S(2)}) collective-permute-start(f32[384,768]{1,0:T(8,128)} %fusion.70), channel_id=1, source_target_pairs={{0,8},{8,0},{16,24},{24,16},{1,9},{9,1},{17,25},{25,17},{2,10},{10... | collective-permute-start | bytes 3538952 | tf_op jit(solution)/shard_map/ppermute | solution.py:476
  555.2 34.4 %collective-permute-start.36 = (f32[384,768]{1,0:T(8,128)}, f32[384,768]{1,0:T(8,128)}, u32[]{:S(2)}, u32[]{:S(2)}) collective-permute-start(f32[384,768]{1,0:T(8,128)} %fusion.74), channel_id=1, source_target_pairs={{0,8},{8,0},{16,24},{24,16},{1,9},{9,1},{17,25},{25,17},{2,10},{10... | collective-permute-start | bytes 3538952 | tf_op jit(solution)/shard_map/ppermute | solution.py:476
  564.6 123.1 %collective-permute-start.48 = (f32[768,768]{1,0:T(8,128)}, f32[768,768]{1,0:T(8,128)}, u32[]{:S(2)}, u32[]{:S(2)}) collective-permute-start(f32[768,768]{1,0:T(8,128)} %add_add_fusion), channel_id=1, source_target_pairs={{0,1},{1,0},{2,3},{3,2},{4,5},{5,4},{6,7},{7,6},{8,9},{9,8},{10,11... | collective-permute-start | bytes 7077896 | tf_op jit(solution)/shard_map/ppermute | solution.py:458
  595.2 31.2 %collective-permute-start.37 = (f16[400,768]{1,0:T(8,128)(2,1)S(1)}, f16[400,768]{1,0:T(8,128)(2,1)}, u32[]{:S(2)}, u32[]{:S(2)}) collective-permute-start(f16[400,768]{1,0:T(8,128)(2,1)S(1)} %pad_maximum_fusion.10), channel_id=1, source_target_pairs={{0,16},{8,24},{16,0},{24,8},{1,17},{9,25},{17,1},{25,9},{2,18},{10... | collective-permute-start | bytes 1843208 | tf_op jit(solution)/shard_map/ppermute | solution.py:476
  622.8 58.6 %collective-permute-start.45 = (f16[112,1536]{1,0:T(8,128)(2,1)}, f16[112,1536]{1,0:T(8,128)(2,1)S(1)}, u32[]{:S(2)}, u32[]{:S(2)}) collective-permute-start(f16[112,1536]{1,0:T(8,128)(2,1)} %get-tuple-element.335), channel_id=1, source_target_pairs={{0,2},{2,4},{4,6},{6,0},{1,3},{3,5},{5,7},{7,1},{8,10},{10,12},{12... | collective-permute-start | bytes 1032200 | tf_op jit(solution)/shard_map/ppermute | solution.py:548
  622.9 58.5 %collective-permute-start.46 = (f16[112,1536]{1,0:T(8,128)(2,1)}, f16[112,1536]{1,0:T(8,128)(2,1)S(1)}, u32[]{:S(2)}, u32[]{:S(2)}) collective-permute-start(f16[112,1536]{1,0:T(8,128)(2,1)} %get-tuple-element.334), channel_id=1, source_target_pairs={{0,4},{2,6},{4,0},{6,2},{1,5},{3,7},{5,1},{7,3},{8,12},{10,14},{12... | collective-permute-start | bytes 1032200 | tf_op jit(solution)/shard_map/ppermute | solution.py:548
  (181 other events, 1620.3 us)
Sparse Core Ops, SparseCore 0:
  10.9 57.5 all-gather.7
  70.8 59.5 all-gather.9
  177.4 57.1 all-gather.5
